TPU v7x, 256 devices: a whole 4x4x8 slice. The times are simulated.
256 devices in a mesh: seq: 64 (over x_hi, y, z), tp: 4 (over x_lo, core).
Axes of the slice: x: 4 (x_hi: 2, x_lo: 2; x = x_hi * 2 + x_lo), y: 4, z: 8, core: 2. Of those that a mesh axis runs over, the one named last changes fastest.
Arguments:
- mixer_input: bfloat16 [8192, 8192], P('seq', 'tp'), may hold values from -6 to 6
- gate_input: bfloat16 [8192, 8192], P('seq', 'tp'), may hold values from -6 to 6
- input_matrix: bfloat16 [8192, 1024], P('seq', 'tp'), may hold values from -6 to 6
- output_matrix: bfloat16 [8192, 1024], P('seq', 'tp'), may hold values from -6 to 6
- step_raw: float32 [8192, 128], P('seq', 'tp'), may hold values from -3 to 3
- step_bias: float32 [128], P('tp'), may hold values from -1 to 0.5
- decay_rate: float32 [128], P('tp'), may hold values from 0.0001 to 0.05
- skip_weight: float32 [128], P('tp'), may hold values from 0.5 to 1.5
- conv_mixer: float32 [4, 8192], P(None, 'tp'), may hold values from -3 to 3
- conv_input: float32 [4, 1024], P(None, 'tp'), may hold values from -3 to 3
- conv_output: float32 [4, 1024], P(None, 'tp'), may hold values from -3 to 3
- norm_gain: float32 [8192], P('tp'), may hold values from 0.5 to 1.5
- queries: bfloat16 [8192, 8192], P('seq', 'tp'), may hold values from -5 to 5
- keys: bfloat16 [8192, 1024], P('seq', 'tp'), may hold values from -5 to 5
- values: bfloat16 [8192, 1024], P('seq', 'tp'), may hold values from -6 to 6
Outputs:
- mixer_out: bfloat16 [8192, 8192], P('seq', 'tp')
- attention_out: bfloat16 [8192, 8192], P('seq', 'tp')
All inputs are finite; a program needn't handle non-finite values.
Results may differ from a plain program's by a relative error of at most 0.007.
Values may be sent and summed in bfloat16 or wider, within the bound.
No kernel may reach another device: no remote copies, remote signals or barrier semaphores. Data moves between devices by JAX's collectives and lax.ppermute only.
A program may use at most 192 MiB of HBM per device.

v0:
```python
import math

import jax
import jax.numpy as jnp
from jax import lax
from jax.sharding import Mesh
from jax.sharding import PartitionSpec as P

MH = 128
P_SIZE = 64
STATE = 128
HD = 128
CONV = 4
SEQ = ("seq_0", "seq_1", "seq_2")


norm_epsilon = 1e-05
lowest_score = -1e30


def from_behind(value, axis, by):
    size = lax.axis_size(axis)
    pairs = [(i, i + by) for i in range(size) if 0 <= i + by < size]
    return lax.ppermute(value, axis, pairs)


def neutral_like(value, identity):
    return jax.tree.map(
        lambda part, zero: jnp.zeros_like(part) + jnp.asarray(zero, part.dtype), value, identity
    )


def entering_2(value, axes, combine, identity):
    before = start = neutral_like(value, identity)
    subtotal = value
    for axis in reversed(axes):
        size, mine = (lax.axis_size(axis), lax.axis_index(axis))
        pieces = jax.tree.map(lambda part: lax.all_gather(part, axis), subtotal)
        inside, subtotal = (start, start)
        for k in range(size):
            passed = k < mine
            subtotal = combine(subtotal, jax.tree.map(lambda part: part[k], pieces))
            inside = jax.tree.map(lambda new, old: jnp.where(passed, new, old), subtotal, inside)
        before = combine(inside, before)
    return before


def from_everyone(value, axis):
    size = lax.axis_size(axis)
    return lax.all_to_all(
        jnp.broadcast_to(value[None], (size, *value.shape)), axis, 0, 0, tiled=True
    )


def taken_together(value, axis):
    return from_everyone(value, axis).sum(axis=0)


def partner(block, axis, distance):
    count = lax.axis_size(axis)
    route = []
    for low in range(count):
        high = low | 1 << distance
        if high != low and high < count:
            route += [(low, high), (high, low)]
    return lax.ppermute(block, axis, route)


def in_one_piece(arrays, axis, dim, along):
    both = jnp.concatenate(arrays, axis=along)
    result, at, gathered = (lax.all_gather(both, axis, axis=dim, tiled=True), 0, [])
    for a in arrays:
        gathered.append(lax.slice_in_dim(result, at, at + a.shape[along], axis=along))
        at += a.shape[along]
    return tuple(gathered)


def conv_silu(raw_rows, weights, history):
    padded = jnp.concatenate([history, raw_rows], axis=0).astype(jnp.float32)
    length = raw_rows.shape[0]
    summed = jnp.zeros((length, raw_rows.shape[1]), jnp.float32)
    for offset in range(weights.shape[0]):
        summed = summed + weights[offset][None, :] * padded[offset : offset + length]
    return jax.nn.silu(summed)


def ssd_block(signal, b_state, c_state, step_size, rates, carried):
    group_heads = signal.shape[1] // b_state.shape[1]
    log_decay = jnp.cumsum(-step_size * rates[None, :], axis=0)
    length = signal.shape[0]
    places = jnp.arange(length, dtype=jnp.int32)
    causal = (places[:, None] >= places[None, :])[:, :, None]
    spread = jnp.where(causal, log_decay[:, None, :] - log_decay[None, :, :], 0.0)
    decays = jnp.where(causal, jnp.exp(spread), 0.0)
    coupling = jnp.einsum("tgn,sgn->gts", c_state, b_state)
    coupling = jnp.repeat(coupling, group_heads, axis=0)
    mixing = jnp.transpose(decays, (2, 0, 1)) * coupling
    scaled = signal * step_size[:, :, None]
    output = jnp.einsum("hts,shp->thp", mixing, scaled)
    b_heads = jnp.repeat(b_state, group_heads, axis=1)
    c_heads = jnp.repeat(c_state, group_heads, axis=1)
    output = output + jnp.exp(log_decay)[:, :, None] * jnp.einsum("thn,hpn->thp", c_heads, carried)
    closing = jnp.exp(log_decay[-1][None, :] - log_decay)
    weighted = scaled * closing[:, :, None]
    updated = jnp.exp(log_decay[-1])[:, None, None] * carried + jnp.einsum(
        "shp,shn->hpn", weighted, b_heads
    )
    return (output, updated, log_decay, c_heads)


def combine_states(earlier, later):
    return (earlier[0] * later[0], later[0][:, None, None] * earlier[1] + later[1])


def attend_update(carry, query_block, query_start, key_block, value_block, key_start):
    maxima, totals, accum = carry
    kv_heads = key_block.shape[1] // HD
    grouped = query_block.shape[1] // HD // kv_heads
    query_rows = query_block.shape[0]
    key_rows = key_block.shape[0]
    query_four = query_block.reshape(query_rows, kv_heads, grouped, HD)
    key_three = key_block.reshape(key_rows, kv_heads, HD)
    value_three = value_block.reshape(key_rows, kv_heads, HD)
    scores = jnp.einsum("qhgd,khd->hgqk", query_four, key_three, preferred_element_type=jnp.float32)
    scores = scores * (1.0 / math.sqrt(HD))
    query_places = query_start + jnp.arange(query_rows, dtype=jnp.int32)
    key_places = key_start + jnp.arange(key_rows, dtype=jnp.int32)
    allowed = key_places[None, :] <= query_places[:, None]
    masked = jnp.where(allowed, scores, lowest_score)
    newmax = jnp.maximum(maxima, jnp.max(masked, axis=-1))
    probs = jnp.where(allowed, jnp.exp(masked - newmax[..., None]), 0.0)
    factor = jnp.exp(maxima - newmax)
    totals = totals * factor + jnp.sum(probs, axis=-1)
    rounded = probs.astype(jnp.bfloat16)
    product = jnp.einsum("hgqk,khd->hgqd", rounded, value_three, preferred_element_type=jnp.float32)
    accum = accum * factor[..., None] + product
    return (newmax, totals, accum)


def finish(carry):
    maxima, totals, accum = carry
    result = accum / totals[..., None]
    result = jnp.transpose(result, (2, 0, 1, 3))
    return result.reshape(result.shape[0], -1).astype(jnp.bfloat16)


def mixer_local(
    mixer_input,
    gate_input,
    input_matrix,
    output_matrix,
    step_raw,
    step_bias,
    decay_rate,
    skip_weight,
    conv_mixer,
    conv_input,
    conv_output,
    norm_gain,
):
    reach = CONV - 1
    history = from_behind(
        (mixer_input[-reach:], input_matrix[-reach:], output_matrix[-reach:]), SEQ, 1
    )
    length = mixer_input.shape[0]
    heads = mixer_input.shape[1] // P_SIZE
    groups = input_matrix.shape[1] // STATE
    signal = conv_silu(mixer_input, conv_mixer, history[0]).reshape(length, heads, P_SIZE)
    b_state = conv_silu(input_matrix, conv_input, history[1]).reshape(length, groups, STATE)
    c_state = conv_silu(output_matrix, conv_output, history[2]).reshape(length, groups, STATE)
    step_size = jax.nn.softplus(step_raw + step_bias[None, :])
    carried = jnp.zeros((heads, P_SIZE, STATE), jnp.float32)
    output, carried, log_decay, c_heads = ssd_block(
        signal, b_state, c_state, step_size, decay_rate, carried
    )
    offset_log = log_decay[-1]
    device_decay = jnp.exp(offset_log)
    identity = (jnp.ones((heads,), jnp.float32), jnp.zeros((heads, P_SIZE, STATE), jnp.float32))
    prefix_decay, entering = entering_2((device_decay, carried), SEQ, combine_states, identity)
    mixed = output
    mixed = mixed + jnp.exp(log_decay)[:, :, None] * jnp.einsum("thn,hpn->thp", c_heads, entering)
    mixed = mixed + skip_weight[None, :, None] * signal
    gated = mixed.reshape(length, heads * P_SIZE) * jax.nn.silu(gate_input.astype(jnp.float32))
    squares = taken_together(jnp.sum(gated * gated, axis=1), "tp")
    scaling = lax.rsqrt(squares / (MH * P_SIZE) + norm_epsilon)
    return (gated * scaling[:, None] * norm_gain[None, :]).astype(jnp.bfloat16)


def attend_local(queries, keys, values):
    length = queries.shape[0]
    half_len = length // 2
    device = lax.axis_index(SEQ)
    count = lax.axis_size(SEQ)
    own_start = device * length
    near_rows = queries[:half_len]
    far_rows = queries[half_len:]
    for bit_index in range(count.bit_length() - 1):
        far_rows = partner(far_rows, SEQ, bit_index)
    far_start = (count - 1 - device) * length + half_len
    kv_heads = keys.shape[1] // HD
    grouped = queries.shape[1] // HD // kv_heads

    def fresh():
        return (
            jnp.full((kv_heads, grouped, half_len), lowest_score, jnp.float32),
            jnp.zeros((kv_heads, grouped, half_len), jnp.float32),
            jnp.zeros((kv_heads, grouped, half_len, HD), jnp.float32),
        )

    key_piece, value_piece = in_one_piece((keys, values), SEQ, 0, 1)
    span = math.gcd(key_piece.shape[0], 512)

    def visit(position, inner):
        key_start = position * span
        key_block = lax.dynamic_slice_in_dim(key_piece, position * span, span, 0)
        value_block = lax.dynamic_slice_in_dim(value_piece, position * span, span, 0)
        near_state = lax.cond(
            key_start <= own_start + half_len - 1,
            lambda carry_in: attend_update(
                carry_in, near_rows, own_start, key_block, value_block, key_start
            ),
            lambda carry_in: carry_in,
            inner[0],
        )
        far_state = lax.cond(
            key_start <= far_start + half_len - 1,
            lambda carry_in: attend_update(
                carry_in, far_rows, far_start, key_block, value_block, key_start
            ),
            lambda carry_in: carry_in,
            inner[1],
        )
        return (near_state, far_state)

    near_state, far_state = lax.fori_loop(0, key_piece.shape[0] // span, visit, (fresh(), fresh()))
    near_out = finish(near_state)
    far_out = finish(far_state)
    for bit_index in range(count.bit_length() - 1):
        far_out = partner(far_out, SEQ, bit_index)
    return jnp.concatenate([near_out, far_out], axis=0)


def shards(
    mixer_input,
    gate_input,
    input_matrix,
    output_matrix,
    step_raw,
    step_bias,
    decay_rate,
    skip_weight,
    conv_mixer,
    conv_input,
    conv_output,
    norm_gain,
    queries,
    keys,
    values,
):
    mixer_out = mixer_local(
        mixer_input,
        gate_input,
        input_matrix,
        output_matrix,
        step_raw,
        step_bias,
        decay_rate,
        skip_weight,
        conv_mixer,
        conv_input,
        conv_output,
        norm_gain,
    )
    attention_out = attend_local(queries, keys, values)
    return (mixer_out, attention_out)


def solution(mesh):
    torus = Mesh(mesh.devices.reshape(2, 4, 8, mesh.shape["tp"]), ("seq_0", "seq_1", "seq_2", "tp"))
    placed = (
        P(SEQ, "tp"),
        P(SEQ, "tp"),
        P(SEQ, "tp"),
        P(SEQ, "tp"),
        P(SEQ, "tp"),
        P("tp"),
        P("tp"),
        P("tp"),
        P(None, "tp"),
        P(None, "tp"),
        P(None, "tp"),
        P("tp"),
        P(SEQ, "tp"),
        P(SEQ, "tp"),
        P(SEQ, "tp"),
    )
    return jax.shard_map(
        shards, mesh=torus, in_specs=placed, out_specs=(P(SEQ, "tp"), P(SEQ, "tp")), check_vma=False
    )
```

profile of v0, /device:TPU:1, one launch (start us, length us, event | category | flops | bytes accessed | tf_op | source)
XLA Modules:
  0.0 486.6 jit_solution(17566430420498591905)
XLA Ops:
  7.9 4.3 collective-permute-start.2
  26.5 12.4 %all-gather.1 = f32[8,1,32]{2,1,0:T(1,128)S(1)} all-gather(f32[1,1,32]{2,1,0:T(1,128)S(1)} %get-tuple-element.504), channel_id=1, replica_groups=mesh['seq_0'=2,'seq_1'=4,'seq_2'=8,'tp'=4] {'seq_2'}, dimensions={0}, use_global_device_ids=true | all-gather | bytes 1152 | tf_op jit(solution)/shard_map/all_gather | solution.py:38
  39.0 82.5 %all-gather.15.cloned.1.call-done = f32[256,64,128]{2,1,0:T(8,128)} async-done(((f32[32,64,128]{2,1,0:T(8,128)}), f32[256,64,128]{2,1,0:T(8,128)}) %all-gather.15.cloned.1.call-update) | async-done | bytes 8388624 | tf_op jit(solution)/shard_map/all_gather | solution.py:38
  121.5 4.6 bitcast_add_fusion.4
  126.4 7.0 %collective-permute-done.3 = bf16[64,2048]{1,0:T(8,128)(2,1)S(1)} collective-permute-done((bf16[64,2048]{1,0:T(8,128)(2,1)S(1)}, bf16[64,2048]{1,0:T(8,128)(2,1)S(1)}, u32[]{:S(2)}, u32[]{:S(2)}) %collective-permute-start.3) | collective-permute-done | bytes 262176 | tf_op jit(solution)/shard_map/ppermute | solution.py:66
  135.2 13.7 %collective-permute-done.4 = bf16[64,2048]{1,0:T(8,128)(2,1)S(1)} collective-permute-done((bf16[64,2048]{1,0:T(8,128)(2,1)S(1)}, bf16[64,2048]{1,0:T(8,128)(2,1)S(1)}, u32[]{:S(2)}, u32[]{:S(2)}) %collective-permute-start.4) | collective-permute-done | bytes 262176 | tf_op jit(solution)/shard_map/ppermute | solution.py:66
  150.9 16.0 %collective-permute-done.5 = bf16[64,2048]{1,0:T(8,128)(2,1)S(1)} collective-permute-done((bf16[64,2048]{1,0:T(8,128)(2,1)S(1)}, bf16[64,2048]{1,0:T(8,128)(2,1)S(1)}, u32[]{:S(2)}, u32[]{:S(2)}) %collective-permute-start.5) | collective-permute-done | bytes 262176 | tf_op jit(solution)/shard_map/ppermute | solution.py:66
  168.0 9.6 %all-gather.2 = f32[4,1,32]{2,1,0:T(1,128)S(1)} all-gather(f32[1,1,32]{2,1,0:T(1,128)S(1)} %fusion.151), channel_id=1, replica_groups=mesh['seq_0'=2,'seq_1'=4,'seq_2'=8,'tp'=4] {'seq_1'}, dimensions={0}, use_global_device_ids=true | all-gather | bytes 640 | tf_op jit(solution)/shard_map/all_gather | solution.py:38
  179.2 5.4 %collective-permute-done.7 = bf16[64,2048]{1,0:T(8,128)(2,1)S(1)} collective-permute-done((bf16[64,2048]{1,0:T(8,128)(2,1)S(1)}, bf16[64,2048]{1,0:T(8,128)(2,1)S(1)}, u32[]{:S(2)}, u32[]{:S(2)}) %collective-permute-start.7) | collective-permute-done | bytes 262176 | tf_op jit(solution)/shard_map/ppermute | solution.py:66
  184.6 4.5 collective-permute-start.8
  189.1 93.2 %all-gather.13.cloned.1.call-done = bf16[8192,512]{1,0:T(8,128)(2,1)} async-done(((bf16[128,512]{1,0:T(8,128)(2,1)}), bf16[8192,512]{1,0:T(8,128)(2,1)}) %all-gather.13.cloned.1.call-update) | async-done | bytes 8388624 | tf_op jit(solution)/shard_map/all_gather | solution.py:71
  282.3 5.8 %fusion.155 = (bf16[8192,256]{1,0:T(8,128)(2,1)}, bf16[8192,256]{1,0:T(8,128)(2,1)}) fusion(bf16[8192,512]{1,0:T(8,128)(2,1)} %all-gather.13.cloned.1.call-done), kind=kLoop, calls=%fused_computation.259 | loop fusion | bytes 16777216 | tf_op jit(solution)/shard_map/slice | solution.py:73
  289.9 90.3 %while.26 = (s32[]{:T(128)}, f32[2,8,64]{2,1,0:T(8,128)S(1)}, f32[2,8,64]{2,1,0:T(8,128)S(1)}, f32[2,8,64,128]{3,2,1,0:T(8,128)}, f32[2,8,64]{2,1,0:T(8,128)S(1)...) while((s32[]{:T(128)}, f32[2,8,64]{2,1,0:T(8,128)S(1)}, ...), condition=%wide.region_12.13_spmd, body=%wide.region_3.12_spmd.sunk | while | flops 551097472 | bytes 20850180 | solution.py:235
  291.0 5.8 %conditional.4 = ((f32[2,8,64]{2,1,0:T(8,128)S(1)}, f32[2,8,64]{2,1,0:T(8,128)S(1)}, f32[2,8,64,128]{3,2,1,0:T(8,128)})) conditional(s32[]{:T(128)} %convert_element_type.102, (f32[2,8,64]{2,1,0:T(8,128)S(1)}, f32[2,8,64]{2,1,0:T(8,128)S(1)}, f32[2,8,64,128]{3,2,1,0:T(8,128)}) %tuple.93, (s32[]{:T(128)}, s32[]{:T(128)}, ...), branch_computations={%region_4.4_spmd, %region_5.7_spmd} | conditional | flops 275548736 | bytes 9900584 | solution.py:217
  296.8 4.2 conditional.5
  302.1 4.2 conditional.5
  312.7 4.2 conditional.5
  323.2 4.2 conditional.5
  328.5 4.2 conditional.5
  333.8 4.2 conditional.5
  339.1 4.2 conditional.5
  344.3 4.2 conditional.5
  349.6 4.2 conditional.5
  360.2 4.2 conditional.5
  370.7 4.2 conditional.5
  393.4 15.1 %all-gather.3 = f32[2,1,32]{2,1,0:T(1,128)S(1)} all-gather(f32[1,1,32]{2,1,0:T(1,128)S(1)} %copy-done.47), channel_id=1, replica_groups=mesh['seq_0'=2,'seq_1'=4,'seq_2'=8,'tp'=4] {'seq_0'}, dimensions={0}, use_global_device_ids=true | all-gather | bytes 384 | tf_op jit(solution)/shard_map/all_gather | solution.py:38
  412.4 5.4 %collective-permute-done.11 = bf16[64,2048]{1,0:T(8,128)(2,1)S(1)} collective-permute-done((bf16[64,2048]{1,0:T(8,128)(2,1)S(1)}, bf16[64,2048]{1,0:T(8,128)(2,1)S(1)}, u32[]{:S(2)}, u32[]{:S(2)}) %collective-permute-start.11) | collective-permute-done | bytes 262176 | tf_op jit(solution)/shard_map/ppermute | solution.py:66
  417.8 4.4 collective-permute-start.12
  426.4 8.8 %collective-permute-start.13 = (bf16[64,2048]{1,0:T(8,128)(2,1)S(1)}, bf16[64,2048]{1,0:T(8,128)(2,1)}, u32[]{:S(2)}, u32[]{:S(2)}) collective-permute-start(bf16[64,2048]{1,0:T(8,128)(2,1)S(1)} %collective-permute-done.12), channel_id=1, source_target_pairs={{0,64},{64,0},{4,68},{68,4},{8,72},{72,8},{12,76},{76,12},{16,80},... | collective-permute-start | bytes 786440 | tf_op jit(solution)/shard_map/ppermute | solution.py:66
  439.3 13.5 %collective-permute-start.14 = (bf16[64,2048]{1,0:T(8,128)(2,1)}, bf16[64,2048]{1,0:T(8,128)(2,1)}, u32[]{:S(2)}, u32[]{:S(2)}) collective-permute-start(bf16[64,2048]{1,0:T(8,128)(2,1)} %collective-permute-done.13), channel_id=1, source_target_pairs={{0,128},{128,0},{4,132},{132,4},{8,136},{136,8},{12,140},{140,12},... | collective-permute-start | bytes 786440 | tf_op jit(solution)/shard_map/ppermute | solution.py:66
  453.0 6.5 %fusion.30 = f32[128,32,64]{0,2,1:T(8,128)S(1)} fusion(bf16[128,32,128]{2,0,1:T(8,128)(2,1)S(1)} %bitcast.291, f32[2,32,64,128]{3,2,1,0:T(8,128)} %all-gather.11.cloned.1.call-done, f32[4,32,64,128]{3,2,1,0:T(8,128)} %all-gather.9.cloned.1.call-done, f32[256,64,128]{2,1,0:T(8,128)} %all-gather.15.cloned.1.call-done, f32[32]{0:T(128)S(1)} %copy-done.45, ...), kind=kOutput, calls=%fused_computation.48 | convolution fusion | flops 78643200 | bytes 16795662 | tf_op jit(solution)/shard_map/thn,hpn->thp/dot_general | solution.py:181
  464.1 11.7 %all-to-all-start = ((f32[4,1,128]{2,1,0:T(1,128)}), f32[4,1,128]{2,1,0:T(1,128)S(1)}, u32[]{:S(2)}, u32[]{:S(2)}) async-start(f32[4,1,128]{2,1,0:T(1,128)} %broadcast_in_dim.91), calls=%async_computation | async-start | bytes 4096 | tf_op jit(solution)/shard_map/all_to_all | solution.py:50
  (427 shorter events, 166.8 us)
Async XLA Ops:
  7.2 114.3 %all-gather.15.cloned.1.call-start = ((), (), s32[]{:S(2)}) async-start(), calls=%async_computation.4 | async-start | bytes 9437184 | tf_op jit(solution)/shard_map/all_gather | solution.py:38
  7.9 12.3 %collective-permute-start.2 = (bf16[3,256]{1,0:T(4,128)(2,1)S(1)}, bf16[3,256]{1,0:T(4,128)(2,1)S(1)}, u32[]{:S(2)}, u32[]{:S(2)}) collective-permute-start(bf16[3,256]{1,0:T(4,128)(2,1)S(1)} %slice.201), channel_id=1, source_target_pairs={{0,4},{4,8},{8,12},{12,16},{16,20},{20,24},{24,28},{28,32},{32,36}... | collective-permute-start | bytes 4616 | tf_op jit(solution)/shard_map/ppermute | solution.py:24
  13.0 8.7 %collective-permute-start = (bf16[3,2048]{1,0:T(4,128)(2,1)S(1)}, bf16[3,2048]{1,0:T(4,128)(2,1)S(1)}, u32[]{:S(2)}, u32[]{:S(2)}) collective-permute-start(bf16[3,2048]{1,0:T(4,128)(2,1)S(1)} %slice.183), channel_id=1, source_target_pairs={{0,4},{4,8},{8,12},{12,16},{16,20},{20,24},{24,28},{28,32},{32,36}... | collective-permute-start | bytes 36872 | tf_op jit(solution)/shard_map/ppermute | solution.py:24
  25.7 256.6 %all-gather.13.cloned.1.call-start = ((), (), s32[]{:S(2)}) async-start(), calls=%async_computation.3 | async-start | bytes 8519680 | tf_op jit(solution)/shard_map/all_gather | solution.py:71
  26.4 353.8 %all-gather.9.cloned.1.call-start = ((), (), s32[]{:S(2)}) async-start(), calls=%async_computation.1 | async-start | bytes 5242880 | tf_op jit(solution)/shard_map/all_gather | solution.py:38
  38.9 129.1 %copy-start.13 = (f32[8,1,32]{2,1,0:T(1,128)}, f32[8,1,32]{2,1,0:T(1,128)S(1)}, u32[]{:S(2)}) copy-start(f32[8,1,32]{2,1,0:T(1,128)S(1)} %all-gather.1) | copy-start | bytes 3076
  38.9 87.2 %copy-start.44 = (f32[32]{0:T(128)}, f32[32]{0:T(128)S(1)}, u32[]{:S(2)}) copy-start(f32[32]{0:T(128)S(1)} %bitcast_multiply_fusion.1) | copy-start | bytes 388
  38.9 87.2 %copy-start.27 = (f32[32]{0:T(128)}, f32[32]{0:T(128)S(1)}, u32[]{:S(2)}) copy-start(f32[32]{0:T(128)S(1)} %get-tuple-element.510) | copy-start | bytes 388
  38.9 87.2 %copy-start.29 = (f32[32]{0:T(128)}, f32[32]{0:T(128)S(1)}, u32[]{:S(2)}) copy-start(f32[32]{0:T(128)S(1)} %get-tuple-element.511) | copy-start | bytes 388
  38.9 87.2 %copy-start.31 = (f32[32]{0:T(128)}, f32[32]{0:T(128)S(1)}, u32[]{:S(2)}) copy-start(f32[32]{0:T(128)S(1)} %get-tuple-element.512) | copy-start | bytes 388
  38.9 87.2 %copy-start.33 = (f32[32]{0:T(128)}, f32[32]{0:T(128)S(1)}, u32[]{:S(2)}) copy-start(f32[32]{0:T(128)S(1)} %get-tuple-element.513) | copy-start | bytes 388
  38.9 87.2 %copy-start.35 = (f32[32]{0:T(128)}, f32[32]{0:T(128)S(1)}, u32[]{:S(2)}) copy-start(f32[32]{0:T(128)S(1)} %get-tuple-element.514) | copy-start | bytes 388
  38.9 87.2 %copy-start.37 = (f32[32]{0:T(128)}, f32[32]{0:T(128)S(1)}, u32[]{:S(2)}) copy-start(f32[32]{0:T(128)S(1)} %get-tuple-element.515) | copy-start | bytes 388
  38.9 87.2 %copy-start.39 = (f32[32]{0:T(128)}, f32[32]{0:T(128)S(1)}, u32[]{:S(2)}) copy-start(f32[32]{0:T(128)S(1)} %get-tuple-element.516) | copy-start | bytes 388
  126.2 326.7 %all-gather.11.cloned.1.call-start = ((), (), s32[]{:S(2)}) async-start(), calls=%async_computation.2 | async-start | bytes 3145728 | tf_op jit(solution)/shard_map/all_gather | solution.py:38
  126.3 7.1 %collective-permute-start.3 = (bf16[64,2048]{1,0:T(8,128)(2,1)S(1)}, bf16[64,2048]{1,0:T(8,128)(2,1)S(1)}, u32[]{:S(2)}, u32[]{:S(2)}) collective-permute-start(bf16[64,2048]{1,0:T(8,128)(2,1)S(1)} %get-tuple-element.500), channel_id=1, source_target_pairs={{0,4},{4,0},{8,12},{12,8},{16,20},{20,16},{24,28},{28,24},{32,36},... | collective-permute-start | bytes 786440 | tf_op jit(solution)/shard_map/ppermute | solution.py:66
  133.4 15.5 %collective-permute-start.4 = (bf16[64,2048]{1,0:T(8,128)(2,1)S(1)}, bf16[64,2048]{1,0:T(8,128)(2,1)S(1)}, u32[]{:S(2)}, u32[]{:S(2)}) collective-permute-start(bf16[64,2048]{1,0:T(8,128)(2,1)S(1)} %collective-permute-done.3), channel_id=1, source_target_pairs={{0,8},{8,0},{4,12},{12,4},{16,24},{24,16},{20,28},{28,20},{32,40},... | collective-permute-start | bytes 786440 | tf_op jit(solution)/shard_map/ppermute | solution.py:66
  148.9 18.0 %collective-permute-start.5 = (bf16[64,2048]{1,0:T(8,128)(2,1)S(1)}, bf16[64,2048]{1,0:T(8,128)(2,1)S(1)}, u32[]{:S(2)}, u32[]{:S(2)}) collective-permute-start(bf16[64,2048]{1,0:T(8,128)(2,1)S(1)} %collective-permute-done.4), channel_id=1, source_target_pairs={{0,16},{16,0},{4,20},{20,4},{8,24},{24,8},{12,28},{28,12},{32,48},... | collective-permute-start | bytes 786440 | tf_op jit(solution)/shard_map/ppermute | solution.py:66
  166.9 10.7 %collective-permute-start.6 = (bf16[64,2048]{1,0:T(8,128)(2,1)S(1)}, bf16[64,2048]{1,0:T(8,128)(2,1)S(1)}, u32[]{:S(2)}, u32[]{:S(2)}) collective-permute-start(bf16[64,2048]{1,0:T(8,128)(2,1)S(1)} %collective-permute-done.5), channel_id=1, source_target_pairs={{0,32},{32,0},{4,36},{36,4},{8,40},{40,8},{12,44},{44,12},{16,48},... | collective-permute-start | bytes 786440 | tf_op jit(solution)/shard_map/ppermute | solution.py:66
  177.5 110.6 %copy-start.15 = (f32[4,1,32]{2,1,0:T(1,128)}, f32[4,1,32]{2,1,0:T(1,128)S(1)}, u32[]{:S(2)}) copy-start(f32[4,1,32]{2,1,0:T(1,128)S(1)} %all-gather.2) | copy-start | bytes 1540
  177.5 7.0 %collective-permute-start.7 = (bf16[64,2048]{1,0:T(8,128)(2,1)S(1)}, bf16[64,2048]{1,0:T(8,128)(2,1)S(1)}, u32[]{:S(2)}, u32[]{:S(2)}) collective-permute-start(bf16[64,2048]{1,0:T(8,128)(2,1)S(1)} %collective-permute-done.6), channel_id=1, source_target_pairs={{0,64},{64,0},{4,68},{68,4},{8,72},{72,8},{12,76},{76,12},{16,80},... | collective-permute-start | bytes 786440 | tf_op jit(solution)/shard_map/ppermute | solution.py:66
  184.6 103.6 %collective-permute-start.8 = (bf16[64,2048]{1,0:T(8,128)(2,1)S(1)}, bf16[64,2048]{1,0:T(8,128)(2,1)S(1)}, u32[]{:S(2)}, u32[]{:S(2)}) collective-permute-start(bf16[64,2048]{1,0:T(8,128)(2,1)S(1)} %collective-permute-done.7), channel_id=1, source_target_pairs={{0,128},{128,0},{4,132},{132,4},{8,136},{136,8},{12,140},{140,12},... | collective-permute-start | bytes 786440 | tf_op jit(solution)/shard_map/ppermute | solution.py:66
  383.8 38.4 %copy-start.3 = (f32[131,256]{1,0:T(8,128)S(1)}, f32[131,256]{1,0:T(8,128)}, u32[]{:S(2)}) copy-start(f32[131,256]{1,0:T(8,128)} %copy-done.2) | copy-start | bytes 402436
  383.8 38.4 %copy-start.19 = (f32[1,256]{1,0:T(1,128)S(1)}, f32[1,256]{1,0:T(1,128)}, u32[]{:S(2)}) copy-start(f32[1,256]{1,0:T(1,128)} %copy-done.18) | copy-start | bytes 3076
  385.6 5.3 %collective-permute-start.9 = (bf16[64,2048]{1,0:T(8,128)(2,1)S(1)}, bf16[64,2048]{1,0:T(8,128)(2,1)S(1)}, u32[]{:S(2)}, u32[]{:S(2)}) collective-permute-start(bf16[64,2048]{1,0:T(8,128)(2,1)S(1)} %bitcast.298), channel_id=1, source_target_pairs={{0,4},{4,0},{8,12},{12,8},{16,20},{20,16},{24,28},{28,24},{32,36},... | collective-permute-start | bytes 786440 | tf_op jit(solution)/shard_map/ppermute | solution.py:66
  386.8 25.6 %collective-permute-start.1 = (bf16[3,256]{1,0:T(4,128)(2,1)S(1)}, bf16[3,256]{1,0:T(4,128)(2,1)S(1)}, u32[]{:S(2)}, u32[]{:S(2)}) collective-permute-start(bf16[3,256]{1,0:T(4,128)(2,1)S(1)} %slice.192), channel_id=1, source_target_pairs={{0,4},{4,8},{8,12},{12,16},{16,20},{20,24},{24,28},{28,32},{32,36}... | collective-permute-start | bytes 4616 | tf_op jit(solution)/shard_map/ppermute | solution.py:24
  390.9 17.6 %collective-permute-start.10 = (bf16[64,2048]{1,0:T(8,128)(2,1)S(1)}, bf16[64,2048]{1,0:T(8,128)(2,1)S(1)}, u32[]{:S(2)}, u32[]{:S(2)}) collective-permute-start(bf16[64,2048]{1,0:T(8,128)(2,1)S(1)} %collective-permute-done.9), channel_id=1, source_target_pairs={{0,8},{8,0},{4,12},{12,4},{16,24},{24,16},{20,28},{28,20},{32,40},... | collective-permute-start | bytes 786440 | tf_op jit(solution)/shard_map/ppermute | solution.py:66
  408.5 9.3 %collective-permute-start.11 = (bf16[64,2048]{1,0:T(8,128)(2,1)S(1)}, bf16[64,2048]{1,0:T(8,128)(2,1)S(1)}, u32[]{:S(2)}, u32[]{:S(2)}) collective-permute-start(bf16[64,2048]{1,0:T(8,128)(2,1)S(1)} %collective-permute-done.10), channel_id=1, source_target_pairs={{0,16},{16,0},{4,20},{20,4},{8,24},{24,8},{12,28},{28,12},{32,48},... | collective-permute-start | bytes 786440 | tf_op jit(solution)/shard_map/ppermute | solution.py:66
  417.8 8.6 %collective-permute-start.12 = (bf16[64,2048]{1,0:T(8,128)(2,1)S(1)}, bf16[64,2048]{1,0:T(8,128)(2,1)S(1)}, u32[]{:S(2)}, u32[]{:S(2)}) collective-permute-start(bf16[64,2048]{1,0:T(8,128)(2,1)S(1)} %collective-permute-done.11), channel_id=1, source_target_pairs={{0,32},{32,0},{4,36},{36,4},{8,40},{40,8},{12,44},{44,12},{16,48},... | collective-permute-start | bytes 786440 | tf_op jit(solution)/shard_map/ppermute | solution.py:66
  426.4 13.0 %collective-permute-start.13 = (bf16[64,2048]{1,0:T(8,128)(2,1)S(1)}, bf16[64,2048]{1,0:T(8,128)(2,1)}, u32[]{:S(2)}, u32[]{:S(2)}) collective-permute-start(bf16[64,2048]{1,0:T(8,128)(2,1)S(1)} %collective-permute-done.12), channel_id=1, source_target_pairs={{0,64},{64,0},{4,68},{68,4},{8,72},{72,8},{12,76},{76,12},{16,80},... | collective-permute-start | bytes 786440 | tf_op jit(solution)/shard_map/ppermute | solution.py:66
  439.3 36.5 %collective-permute-start.14 = (bf16[64,2048]{1,0:T(8,128)(2,1)}, bf16[64,2048]{1,0:T(8,128)(2,1)}, u32[]{:S(2)}, u32[]{:S(2)}) collective-permute-start(bf16[64,2048]{1,0:T(8,128)(2,1)} %collective-permute-done.13), channel_id=1, source_target_pairs={{0,128},{128,0},{4,132},{132,4},{8,136},{136,8},{12,140},{140,12},... | collective-permute-start | bytes 786440 | tf_op jit(solution)/shard_map/ppermute | solution.py:66
  464.1 14.7 %all-to-all-start = ((f32[4,1,128]{2,1,0:T(1,128)}), f32[4,1,128]{2,1,0:T(1,128)S(1)}, u32[]{:S(2)}, u32[]{:S(2)}) async-start(f32[4,1,128]{2,1,0:T(1,128)} %broadcast_in_dim.91), calls=%async_computation | async-start | bytes 4096 | tf_op jit(solution)/shard_map/all_to_all | solution.py:50
  (37 other events, 636.0 us)
Sparse Core Ops, SparseCore 0:
  25.8 95.6 all-gather.14
  125.8 156.4 all-gather.12
  284.1 50.4 all-gather.8
  384.0 63.4 all-gather.10
where the time goes:
time: 489 us; the launch traced here: 487 us
  waiting for transfers between devices  232 us (47%)
  starting transfers between devices  66.1 us (14%)
  matrix products  65.1 us (13%)
  blocking collectives  37 us (8%)
  local copies, waits for them, and re-layouts  36 us (7%)
  other arithmetic  33.9 us (7%)
  between operations  14.6 us (3%)
    all_gather x1, waiting for transfers between devices, in_one_piece(): lax.all_gather(both, axis, axis=dim, tiled=True)  93.2 us
    all_gather x3, waiting for transfers between devices, entering_2(): pieces = jax.tree.map(lambda part: lax.all_gather(part, axis), subtotal)  82.5 us
    ppermute x12, waiting for transfers between devices, partner(): return lax.ppermute(block, axis, route)  55 us
    ppermute x12, starting transfers between devices, partner(): return lax.ppermute(block, axis, route)  44 us
    dot_general x17, matrix products, attend_update(): jnp.einsum('hgqk,khd->hgqd', rounded, value_three, preferred_element_type...  43.9 us
    all_gather x3, blocking collectives, entering_2(): pieces = jax.tree.map(lambda part: lax.all_gather(part, axis), subtotal)  37 us
    dynamic_slice x16, local copies, waits for them, and re-layouts, visit(): lax.dynamic_slice_in_dim(value_piece, position * span, span, 0)  17 us
    reduce_sum x17, other arithmetic, attend_update(): totals = totals * factor + jnp.sum(probs, axis=-1)  11.7 us
  transfers between devices with their start and end apart: 20, of which 11 were waited for; matrix products, arithmetic and copies ran while one was open for 26% of the time, Pallas kernels for 0%

commit v1 on v0

v1 whole, which is shorter than its diff:
```python
import math

import jax
import jax.numpy as jnp
from jax import lax
from jax.experimental import pallas as pl
from jax.experimental.pallas import tpu as pltpu
from jax.sharding import Mesh
from jax.sharding import PartitionSpec as P

MH = 128
P_SIZE = 64
STATE = 128
HD = 128
CONV = 4
LINE = ("xh", "y")
SEQ = ("xh", "y", "z")

norm_epsilon = 1e-05
lowest_score = -1e30
EXP2_SCALE = math.log2(math.e) / math.sqrt(HD)


def conv_silu(raw_rows, weights, history):
    padded = jnp.concatenate([history, raw_rows], axis=0).astype(jnp.float32)
    length = raw_rows.shape[0]
    summed = jnp.zeros((length, raw_rows.shape[1]), jnp.float32)
    for offset in range(weights.shape[0]):
        summed = summed + weights[offset][None, :] * padded[offset : offset + length]
    return jax.nn.silu(summed)


def attend_kernel(z_ref, q_ref, kv_ref, o_ref):
    lines, zs, length = q_ref.shape[0], kv_ref.shape[0], q_ref.shape[1]
    span = zs * length
    rows = 2 * length

    def chunk(g):
        both = kv_ref[:, g].reshape(span, 2 * HD)
        return both[:, :HD], both[:, HD:]

    def scores_of(q, k):
        return lax.dot_general(q, k, (((1,), (1,)), ((), ())), preferred_element_type=jnp.float32)

    def one_line(g, _):
        both = q_ref[g, :, : 2 * HD]
        q = jnp.concatenate([both[:, :HD], both[:, HD:]], axis=0)
        k, v = chunk(g)
        s = scores_of(q, k)
        place = lax.broadcasted_iota(jnp.int32, (rows, span), 0) % length + z_ref[0] * length
        key_place = lax.broadcasted_iota(jnp.int32, (rows, span), 1)
        s = jnp.where(key_place <= place, s, lowest_score)
        m = jnp.max(s, axis=-1, keepdims=True)
        p = jnp.exp2((s - m) * EXP2_SCALE)
        total = jnp.sum(p, axis=-1, keepdims=True)
        acc = jnp.dot(p.astype(jnp.bfloat16), v, preferred_element_type=jnp.float32)

        def visit(other, carry):
            m, total, acc = carry
            k, v = chunk(other)
            s = scores_of(q, k)
            new = jnp.maximum(m, jnp.max(s, axis=-1, keepdims=True))
            p = jnp.exp2((s - new) * EXP2_SCALE)
            factor = jnp.exp2((m - new) * EXP2_SCALE)
            total = total * factor + jnp.sum(p, axis=-1, keepdims=True)
            acc = acc * factor + jnp.dot(
                p.astype(jnp.bfloat16), v, preferred_element_type=jnp.float32
            )
            return new, total, acc

        m, total, acc = lax.fori_loop(0, g, visit, (m, total, acc))
        out = (acc / total).astype(jnp.bfloat16)
        o_ref[g, :, :HD] = out[:length]
        o_ref[g, :, HD:] = out[length:]
        return 0

    lax.fori_loop(0, lines, one_line, 0)


def attend(z, q, kv):
    lines, length = q.shape[0], q.shape[1]
    pairs = lines * (lines + 1) // 2 * 2 * length * kv.shape[0] * length
    return pl.pallas_call(
        attend_kernel,
        out_shape=jax.ShapeDtypeStruct((lines, length, 2 * HD), jnp.bfloat16),
        in_specs=[
            pl.BlockSpec(memory_space=pltpu.SMEM),
            pl.BlockSpec(memory_space=pltpu.VMEM),
            pl.BlockSpec(memory_space=pltpu.VMEM),
        ],
        out_specs=pl.BlockSpec(memory_space=pltpu.VMEM),
        cost_estimate=pl.CostEstimate(
            flops=pairs * HD * 4, bytes_accessed=kv.size * 2 + q.size * 4, transcendentals=pairs
        ),
        compiler_params=pltpu.CompilerParams(vmem_limit_bytes=40 * 1024 * 1024),
        name="attend",
    )(z, q, kv)


def attend_local(queries, keys, values):
    length = queries.shape[0]
    lines = lax.axis_size(LINE)
    kv_heads = keys.shape[1] // HD
    shared = lines // kv_heads
    q = queries.reshape(length, lines, 2 * HD).transpose(1, 0, 2)
    k = keys.reshape(length, kv_heads, HD).transpose(1, 0, 2)
    v = values.reshape(length, kv_heads, HD).transpose(1, 0, 2)
    kv = jnp.repeat(jnp.concatenate([k, v], axis=2), shared, axis=0)
    kv = lax.all_to_all(kv, LINE, 0, 0, tiled=True)
    kv = lax.all_gather(kv, "z")
    q = lax.all_to_all(q, LINE, 0, 0, tiled=True)
    z = lax.axis_index("z").astype(jnp.int32).reshape(1)
    out = attend(z, q, kv)
    out = lax.all_to_all(out, LINE, 0, 0, tiled=True)
    return out.transpose(1, 0, 2).reshape(length, lines * 2 * HD)


def carry_kernel(piece_ref, o_ref):
    count, rows = o_ref.shape[0], o_ref.shape[1]

    def step(j, state):
        o_ref[j] = state.astype(jnp.bfloat16)
        block = piece_ref[j].astype(jnp.float32)
        log = block[rows : rows + 1] + block[rows + 1 : rows + 2] + block[rows + 2 : rows + 3]
        return jnp.exp(log) * state + block[:rows]

    lax.fori_loop(0, count, step, jnp.zeros((rows, STATE), jnp.float32), unroll=8)


def carry_states(pieces):
    count, rows = pieces.shape[0], pieces.shape[1] - 8
    return pl.pallas_call(
        carry_kernel,
        out_shape=jax.ShapeDtypeStruct((count, rows, STATE), jnp.bfloat16),
        in_specs=[pl.BlockSpec(memory_space=pltpu.VMEM)],
        out_specs=pl.BlockSpec(memory_space=pltpu.VMEM),
        cost_estimate=pl.CostEstimate(
            flops=1000000, bytes_accessed=pieces.size * 4, transcendentals=count * 128
        ),
        name="carry_states",
    )(pieces)


def entering_state(own, log_total):
    heads = own.shape[0]
    count = lax.axis_size(SEQ)
    rows = heads * P_SIZE // count
    per_head = count // heads
    body = own.astype(jnp.bfloat16).reshape(count, rows, STATE)
    log = jnp.repeat(log_total, per_head)[:, None, None]
    high = log.astype(jnp.bfloat16)
    rest = log - high.astype(jnp.float32)
    mid = rest.astype(jnp.bfloat16)
    low = (rest - mid.astype(jnp.float32)).astype(jnp.bfloat16)
    which = lax.broadcasted_iota(jnp.int32, (count, 8, STATE), 1)
    zero = jnp.zeros((), jnp.bfloat16)
    tail = jnp.where(which == 0, high, jnp.where(which == 1, mid, jnp.where(which == 2, low, zero)))
    pieces = lax.all_to_all(jnp.concatenate([body, tail], axis=1), SEQ, 0, 0, tiled=True)
    entering = carry_states(pieces)
    entering = lax.all_to_all(entering, SEQ, 0, 0, tiled=True)
    return entering.reshape(heads, P_SIZE, STATE)


def summed_over_tp(value):
    size = lax.axis_size("tp")
    spread = jnp.broadcast_to(value[None], (size, *value.shape))
    return lax.all_to_all(spread, "tp", 0, 0, tiled=True).sum(axis=0)


def mixer_local(
    mixer_input,
    gate_input,
    input_matrix,
    output_matrix,
    step_raw,
    step_bias,
    decay_rate,
    skip_weight,
    conv_mixer,
    conv_input,
    conv_output,
    norm_gain,
):
    reach = CONV - 1
    length, width = mixer_input.shape
    heads = width // P_SIZE
    groups = input_matrix.shape[1] // STATE
    shared = heads // groups
    count = lax.axis_size(SEQ)
    edge = jnp.concatenate(
        [mixer_input[-reach:], input_matrix[-reach:], output_matrix[-reach:]], axis=1
    )
    edge = lax.ppermute(edge, SEQ, [(i, i + 1) for i in range(count - 1)])
    mid = width + input_matrix.shape[1]
    signal = conv_silu(mixer_input, conv_mixer, edge[:, :width]).reshape(length, heads, P_SIZE)
    b_state = conv_silu(input_matrix, conv_input, edge[:, width:mid])
    c_state = conv_silu(output_matrix, conv_output, edge[:, mid:])
    b_state = b_state.reshape(length, groups, STATE)
    c_state = c_state.reshape(length, groups, STATE)
    step_size = jax.nn.softplus(step_raw + step_bias[None, :])
    places = jnp.arange(length, dtype=jnp.int32)
    causal = places[:, None] >= places[None, :]
    log_decay = jnp.cumsum(-step_size * decay_rate[None, :], axis=0)
    by_head = log_decay.T
    spread = jnp.where(causal, by_head[:, :, None] - by_head[:, None, :], 0.0)
    decays = jnp.where(causal, jnp.exp(spread), 0.0)
    coupling = jnp.einsum("tgn,sgn->gts", c_state, b_state)
    mixing = decays * jnp.repeat(coupling, shared, axis=0)
    scaled = signal * step_size[:, :, None]
    closing = jnp.exp(log_decay[-1][None, :] - log_decay)
    weighted = (scaled * closing[:, :, None]).reshape(length, groups, shared * P_SIZE)
    own = jnp.einsum("sgq,sgn->gqn", weighted, b_state).reshape(heads, P_SIZE, STATE)
    entering = entering_state(own, log_decay[-1])
    output = jnp.einsum("hts,shp->thp", mixing, scaled)
    later = jnp.einsum(
        "tgn,gqn->tgq",
        c_state.astype(jnp.bfloat16),
        entering.reshape(groups, shared * P_SIZE, STATE),
        preferred_element_type=jnp.float32,
    ).reshape(length, heads, P_SIZE)
    mixed = output + jnp.exp(log_decay)[:, :, None] * later
    mixed = mixed + skip_weight[None, :, None] * signal
    gated = mixed.reshape(length, width) * jax.nn.silu(gate_input.astype(jnp.float32))
    squares = summed_over_tp(jnp.sum(gated * gated, axis=1))
    scaling = lax.rsqrt(squares / (MH * P_SIZE) + norm_epsilon)
    return (gated * scaling[:, None] * norm_gain[None, :]).astype(jnp.bfloat16)


def shards(
    mixer_input,
    gate_input,
    input_matrix,
    output_matrix,
    step_raw,
    step_bias,
    decay_rate,
    skip_weight,
    conv_mixer,
    conv_input,
    conv_output,
    norm_gain,
    queries,
    keys,
    values,
):
    attention_out = attend_local(queries, keys, values)
    mixer_out = mixer_local(
        mixer_input,
        gate_input,
        input_matrix,
        output_matrix,
        step_raw,
        step_bias,
        decay_rate,
        skip_weight,
        conv_mixer,
        conv_input,
        conv_output,
        norm_gain,
    )
    return (mixer_out, attention_out)


def solution(mesh):
    torus = Mesh(mesh.devices.reshape(2, 4, 8, mesh.shape["tp"]), ("xh", "y", "z", "tp"))
    placed = (
        P(SEQ, "tp"),
        P(SEQ, "tp"),
        P(SEQ, "tp"),
        P(SEQ, "tp"),
        P(SEQ, "tp"),
        P("tp"),
        P("tp"),
        P("tp"),
        P(None, "tp"),
        P(None, "tp"),
        P(None, "tp"),
        P("tp"),
        P(SEQ, "tp"),
        P(SEQ, "tp"),
        P(SEQ, "tp"),
    )
    return jax.shard_map(
        shards, mesh=torus, in_specs=placed, out_specs=(P(SEQ, "tp"), P(SEQ, "tp")), check_vma=False
    )
```

time: 489 us -> 182 us (0.37)
  waiting for transfers between devices: 232 us -> 44.9 us
  matrix products: 65.1 us -> 1.57 us
  starting transfers between devices: 66.1 us -> 34.6 us
  other arithmetic: 33.9 us -> 4.37 us
  Pallas kernels: 0 us -> 28.4 us
  local copies, waits for them, and re-layouts: 36 us -> 11.9 us
    all_gather x4 -> x1, waiting for transfers between devices: 176 us -> 0.01 us  [attend_local(): kv = lax.all_gather(kv, 'z')]
    dot_general x39 -> x4, matrix products: 65.1 us -> 1.57 us  [the longest x1 0.84 us: mixer_local(): output = jnp.einsum('hts,shp->thp', mixing, scaled)]
    ppermute x15 -> x1, waiting for transfers between devices: 55 us -> 0.01 us  [mixer_local(): edge = lax.ppermute(edge, SEQ, [(i, i + 1) for i in range(count - 1)])]
    ppermute x15 -> x1, starting transfers between devices: 54.2 us -> 3.54 us  [mixer_local(): edge = lax.ppermute(edge, SEQ, [(i, i + 1) for i in range(count - 1)])]
    all_to_all x1 -> x5, waiting for transfers between devices: 1.22 us -> 44.9 us  [the longest x1 22.3 us: entering_state(): entering = lax.all_to_all(entering, SEQ, 0, 0, tiled=True)]
    all_to_all x0 -> x1, blocking collectives: none -> 40.7 us  [entering_state(): lax.all_to_all(jnp.concatenate([body, tail], axis=1), SEQ, 0, 0, tiled=True)]
    all_gather x3 -> x0, blocking collectives: 37 us -> none  [entering_2(): pieces = jax.tree.map(lambda part: lax.all_gather(part, axis), subtotal)]
    pallas_call x0 -> x2, Pallas kernels: none -> 28.4 us  [the longest x1 26.3 us: attend(): pl.pallas_call(attend_kernel, out_shape=jax.ShapeDtypeStruct((lines, leng...]
  transfers between devices with their start and end apart: 20 -> 7, of which waited for: 11 -> 5; matrix products, arithmetic and copies ran while one was open for 26% -> 6% of each run, Pallas kernels for 0% -> 1%
where the time goes in v1:
time: 182 us; the launch traced here: 181 us
  waiting for transfers between devices  44.9 us (25%)
  blocking collectives  40.7 us (22%)
  starting transfers between devices  34.6 us (19%)
  Pallas kernels  28.4 us (16%)
  between operations  14.5 us (8%)
  local copies, waits for them, and re-layouts  11.9 us (7%)
  other arithmetic  4.37 us (2%)
    all_to_all x1, blocking collectives, entering_state(): lax.all_to_all(jnp.concatenate([body, tail], axis=1), SEQ, 0, 0, tiled=True)  40.7 us
    pallas_call x1, Pallas kernels, attend(): pl.pallas_call(attend_kernel, out_shape=jax.ShapeDtypeStruct((lines, leng...  26.3 us
    all_to_all x1, waiting for transfers between devices, entering_state(): entering = lax.all_to_all(entering, SEQ, 0, 0, tiled=True)  22.3 us
    all_to_all x1, waiting for transfers between devices, attend_local(): q = lax.all_to_all(q, LINE, 0, 0, tiled=True)  8.98 us
    all_to_all x1, waiting for transfers between devices, attend_local(): out = lax.all_to_all(out, LINE, 0, 0, tiled=True)  7.87 us
    all_to_all x1, starting transfers between devices, attend_local(): kv = lax.all_to_all(kv, LINE, 0, 0, tiled=True)  7.47 us
    all_to_all x1, starting transfers between devices, entering_state(): entering = lax.all_to_all(entering, SEQ, 0, 0, tiled=True)  7.34 us
    all_to_all x1, starting transfers between devices, summed_over_tp(): return lax.all_to_all(spread, 'tp', 0, 0, tiled=True).sum(axis=0)  6.7 us
  transfers between devices with their start and end apart: 7, of which 5 were waited for; matrix products, arithmetic and copies ran while one was open for 6% of the time, Pallas kernels for 1%

profile of v1, /device:TPU:1, one launch (start us, length us, event | category | flops | bytes accessed | tf_op | source)
XLA Modules:
  0.0 180.9 jit_solution(14434616624840224802)
XLA Ops:
  7.2 0.9 reshape.130
  8.2 0.9 reshape.131
  9.2 0.8 broadcast_in_dim.73
  10.0 7.5 %all-to-all-start.4 = ((bf16[8,128,256]{2,1,0:T(8,128)(2,1)}), bf16[8,128,256]{2,1,0:T(8,128)(2,1)S(1)}, u32[]{:S(2)}, u32[]{:S(2)}) async-start(bf16[8,128,256]{2,1,0:T(8,128)(2,1)} %bitcast.31), calls=%async_computation.4 | async-start | bytes 1048576 | tf_op jit(solution)/shard_map/all_to_all | solution.py:109
  17.6 3.5 %collective-permute-start = (bf16[3,2560]{1,0:T(4,128)(2,1)S(1)}, bf16[3,2560]{1,0:T(4,128)(2,1)S(1)}, u32[]{:S(2)}, u32[]{:S(2)}) collective-permute-start(bf16[3,2560]{1,0:T(4,128)(2,1)S(1)} %pad_maximum_fusion.2), channel_id=1, source_target_pairs={{0,4},{4,8},{8,12},{12,16},{16,20},{20,24},{24,28},{28,32},{32,36}... | collective-permute-start | bytes 46088 | tf_op jit(solution)/shard_map/ppermute | solution.py:193
  21.6 4.9 %all-to-all-done.4 = bf16[8,128,256]{2,1,0:T(8,128)(2,1)S(1)} async-done(((bf16[8,128,256]{2,1,0:T(8,128)(2,1)}), bf16[8,128,256]{2,1,0:T(8,128)(2,1)S(1)}, u32[]{:S(2)}, u32[]{:S(2)}) %all-to-all-start.4) | async-done | bytes 524320 | tf_op jit(solution)/shard_map/all_to_all | solution.py:109
  26.5 0.8 copy-done.2
  28.2 0.6 divide_multiply_fusion
  28.8 0.3 copy.81
  30.0 40.7 %all_to_all.31.piece_ref = bf16[64,40,128]{2,1,0:T(8,128)(2,1)} all-to-all(bf16[64,40,128]{2,1,0:T(8,128)(2,1)S(1)} %pad_maximum_fusion), channel_id=1, replica_groups=mesh['xh'=2,'y'=4,'z'=8,'tp'=4] {'xh','y','z'}, dimensions={0} | all-to-all | bytes 1310720 | tf_op jit(solution)/shard_map/all_to_all | solution.py:158
  70.7 2.1 %carry_states.1 = bf16[64,32,128]{2,1,0:T(8,128)(2,1)} custom-call(bf16[64,40,128]{2,1,0:T(8,128)(2,1)} %all_to_all.31.piece_ref), custom_call_target="tpu_custom_call" | custom-call | flops 1000000 | bytes 1310720 | tf_op jit(solution)/shard_map/carry_states/pallas_call | solution.py:132
  72.8 7.3 %all-to-all-start.1 = ((bf16[64,32,128]{2,1,0:T(8,128)(2,1)}), bf16[64,32,128]{2,1,0:T(8,128)(2,1)S(1)}, u32[]{:S(2)}, u32[]{:S(2)}) async-start(bf16[64,32,128]{2,1,0:T(8,128)(2,1)} %carry_states.1), calls=%async_computation.1 | async-start | bytes 1048576 | tf_op jit(solution)/shard_map/all_to_all | solution.py:160
  80.7 0.7 bitcast_multiply_fusion
  81.4 22.3 %all-to-all-done.1 = bf16[64,32,128]{2,1,0:T(8,128)(2,1)S(1)} async-done(((bf16[64,32,128]{2,1,0:T(8,128)(2,1)}), bf16[64,32,128]{2,1,0:T(8,128)(2,1)S(1)}, u32[]{:S(2)}, u32[]{:S(2)}) %all-to-all-start.1) | async-done | bytes 524320 | tf_op jit(solution)/shard_map/all_to_all | solution.py:160
  103.7 0.3 fusion.24
  104.0 0.8 fusion.1
  104.9 0.3 copy.92
  105.2 0.7 copy-done.1
  105.9 0.4 multiply_reduce_fusion
  106.3 0.6 broadcast_in_dim.72
  106.9 6.7 %all-to-all-start.2 = ((f32[4,1,128]{2,1,0:T(1,128)}), f32[4,1,128]{2,1,0:T(1,128)S(1)}, u32[]{:S(2)}, u32[]{:S(2)}) async-start(f32[4,1,128]{2,1,0:T(1,128)} %broadcast_in_dim.72), calls=%async_computation.2 | async-start | bytes 4096 | tf_op jit(solution)/shard_map/all_to_all | solution.py:167
  113.6 1.3 copy.94
  114.9 1.0 copy.95
  116.0 0.8 all-to-all-done.2
  116.7 4.0 %all-to-all-start.3 = ((bf16[8,128,256]{2,1,0:T(8,128)(2,1)}), bf16[8,128,256]{2,1,0:T(8,128)(2,1)S(1)}, u32[]{:S(2)}, u32[]{:S(2)}) async-start(bf16[8,128,256]{2,1,0:T(8,128)(2,1)} %bitcast.28), calls=%async_computation.3 | async-start | bytes 1048576 | tf_op jit(solution)/shard_map/all_to_all | solution.py:111
  120.7 9.0 %all-to-all-done.3.q_ref = bf16[8,128,256]{2,1,0:T(8,128)(2,1)S(1)} async-done(((bf16[8,128,256]{2,1,0:T(8,128)(2,1)}), bf16[8,128,256]{2,1,0:T(8,128)(2,1)S(1)}, u32[]{:S(2)}, u32[]{:S(2)}) %all-to-all-start.3) | async-done | bytes 524320 | tf_op jit(solution)/shard_map/all_to_all | solution.py:111
  129.7 2.2 %copy-done = bf16[64,128,256]{2,1,0:T(8,128)(2,1)S(1)} copy-done((bf16[64,128,256]{2,1,0:T(8,128)(2,1)S(1)}, bf16[64,128,256]{2,1,0:T(8,128)(2,1)}, u32[]{:S(2)}) %copy-start) | copy-done | bytes 4194328
  131.9 26.3 %attend.1 = bf16[8,128,256]{2,1,0:T(8,128)(2,1)} custom-call(s32[1]{0:T(128)} %bitcast.26.z_ref, bf16[8,128,256]{2,1,0:T(8,128)(2,1)S(1)} %all-to-all-done.3.q_ref, bf16[8,8,128,256]{3,2,1,0:T(8,128)(2,1)S(1)} %bitcast.66), custom_call_target="tpu_custom_call" | custom-call | flops 4831838208 | bytes 5242880 | tf_op jit(solution)/shard_map/attend/pallas_call | solution.py:83
  158.2 5.5 %all-to-all-start.5 = ((bf16[8,128,256]{2,1,0:T(8,128)(2,1)}), bf16[8,128,256]{2,1,0:T(8,128)(2,1)S(1)}, u32[]{:S(2)}, u32[]{:S(2)}) async-start(bf16[8,128,256]{2,1,0:T(8,128)(2,1)} %attend.1), calls=%async_computation.5 | async-start | bytes 1048576 | tf_op jit(solution)/shard_map/all_to_all | solution.py:114
  163.7 1.2 multiply_convert_fusion
  164.9 7.9 %all-to-all-done.5 = bf16[8,128,256]{2,1,0:T(8,128)(2,1)S(1)} async-done(((bf16[8,128,256]{2,1,0:T(8,128)(2,1)}), bf16[8,128,256]{2,1,0:T(8,128)(2,1)S(1)}, u32[]{:S(2)}, u32[]{:S(2)}) %all-to-all-start.5) | async-done | bytes 524320 | tf_op jit(solution)/shard_map/all_to_all | solution.py:114
  173.0 1.0 copy.98
  (69 shorter events, 2.9 us)
Async XLA Ops:
  7.2 10.4 %copy-start.3 = (bf16[128,2048]{1,0:T(8,128)(2,1)S(1)}, bf16[128,2048]{1,0:T(8,128)(2,1)}, u32[]{:S(2)}) copy-start(bf16[128,2048]{1,0:T(8,128)(2,1)} %param.15) | copy-start | bytes 1572868
  7.2 10.4 %copy-start.4 = (bf16[128,256]{1,0:T(8,128)(2,1)S(1)}, bf16[128,256]{1,0:T(8,128)(2,1)}, u32[]{:S(2)}) copy-start(bf16[128,256]{1,0:T(8,128)(2,1)} %param.17) | copy-start | bytes 196612
  7.2 10.4 %copy-start.5 = (bf16[128,256]{1,0:T(8,128)(2,1)S(1)}, bf16[128,256]{1,0:T(8,128)(2,1)}, u32[]{:S(2)}) copy-start(bf16[128,256]{1,0:T(8,128)(2,1)} %param.18) | copy-start | bytes 196612
  7.2 14.0 %copy-start.7 = (f32[128,32]{0,1:T(8,128)S(1)}, f32[128,32]{0,1:T(8,128)}, u32[]{:S(2)}) copy-start(f32[128,32]{0,1:T(8,128)} %param.19) | copy-start | bytes 49156
  7.2 14.0 %copy-start.12 = (f32[32]{0:T(128)S(1)}, f32[32]{0:T(128)}, u32[]{:S(2)}) copy-start(f32[32]{0:T(128)} %param.20) | copy-start | bytes 388
  7.2 14.0 %copy-start.11 = (f32[32]{0:T(128)S(1)}, f32[32]{0:T(128)}, u32[]{:S(2)}) copy-start(f32[32]{0:T(128)} %param.21) | copy-start | bytes 388
  7.2 20.7 %copy-start.6 = (f32[4,2048]{1,0:T(4,128)S(1)}, f32[4,2048]{1,0:T(4,128)}, u32[]{:S(2)}) copy-start(f32[4,2048]{1,0:T(4,128)} %param.23) | copy-start | bytes 98308
  7.2 20.7 %copy-start.9 = (f32[4,256]{1,0:T(4,128)S(1)}, f32[4,256]{1,0:T(4,128)}, u32[]{:S(2)}) copy-start(f32[4,256]{1,0:T(4,128)} %param.24) | copy-start | bytes 12292
  10.0 16.5 %all-to-all-start.4 = ((bf16[8,128,256]{2,1,0:T(8,128)(2,1)}), bf16[8,128,256]{2,1,0:T(8,128)(2,1)S(1)}, u32[]{:S(2)}, u32[]{:S(2)}) async-start(bf16[8,128,256]{2,1,0:T(8,128)(2,1)} %bitcast.31), calls=%async_computation.4 | async-start | bytes 1048576 | tf_op jit(solution)/shard_map/all_to_all | solution.py:109
  17.5 112.2 %all-gather.3.cloned.1.call-start = ((), (), s32[]{:S(2)}) async-start(), calls=%async_computation.6 | async-start | bytes 4718592 | tf_op jit(solution)/shard_map/all_gather | solution.py:110
  17.6 10.4 %collective-permute-start = (bf16[3,2560]{1,0:T(4,128)(2,1)S(1)}, bf16[3,2560]{1,0:T(4,128)(2,1)S(1)}, u32[]{:S(2)}, u32[]{:S(2)}) collective-permute-start(bf16[3,2560]{1,0:T(4,128)(2,1)S(1)} %pad_maximum_fusion.2), channel_id=1, source_target_pairs={{0,4},{4,8},{8,12},{12,16},{16,20},{20,24},{24,28},{28,32},{32,36}... | collective-permute-start | bytes 46088 | tf_op jit(solution)/shard_map/ppermute | solution.py:193
  26.5 0.8 copy-start.2
  30.0 50.4 %copy-start.10 = (f32[4,256]{1,0:T(4,128)S(1)}, f32[4,256]{1,0:T(4,128)}, u32[]{:S(2)}) copy-start(f32[4,256]{1,0:T(4,128)} %param.25) | copy-start | bytes 12292
  72.8 30.9 %all-to-all-start.1 = ((bf16[64,32,128]{2,1,0:T(8,128)(2,1)}), bf16[64,32,128]{2,1,0:T(8,128)(2,1)S(1)}, u32[]{:S(2)}, u32[]{:S(2)}) async-start(bf16[64,32,128]{2,1,0:T(8,128)(2,1)} %carry_states.1), calls=%async_computation.1 | async-start | bytes 1048576 | tf_op jit(solution)/shard_map/all_to_all | solution.py:160
  80.2 23.9 %copy-start.13 = (f32[32]{0:T(128)S(1)}, f32[32]{0:T(128)}, u32[]{:S(2)}) copy-start(f32[32]{0:T(128)} %param.22) | copy-start | bytes 388
  104.9 1.0 copy-start.1
  106.9 9.8 %all-to-all-start.2 = ((f32[4,1,128]{2,1,0:T(1,128)}), f32[4,1,128]{2,1,0:T(1,128)S(1)}, u32[]{:S(2)}, u32[]{:S(2)}) async-start(f32[4,1,128]{2,1,0:T(1,128)} %broadcast_in_dim.72), calls=%async_computation.2 | async-start | bytes 4096 | tf_op jit(solution)/shard_map/all_to_all | solution.py:167
  116.7 13.0 %all-to-all-start.3 = ((bf16[8,128,256]{2,1,0:T(8,128)(2,1)}), bf16[8,128,256]{2,1,0:T(8,128)(2,1)S(1)}, u32[]{:S(2)}, u32[]{:S(2)}) async-start(bf16[8,128,256]{2,1,0:T(8,128)(2,1)} %bitcast.28), calls=%async_computation.3 | async-start | bytes 1048576 | tf_op jit(solution)/shard_map/all_to_all | solution.py:111
  129.7 2.2 %copy-start = (bf16[64,128,256]{2,1,0:T(8,128)(2,1)S(1)}, bf16[64,128,256]{2,1,0:T(8,128)(2,1)}, u32[]{:S(2)}) copy-start(bf16[64,128,256]{2,1,0:T(8,128)(2,1)} %all-gather.3.cloned.1.call-done) | copy-start | bytes 12582916
  131.9 31.8 %copy-start.8 = (f32[2048]{0:T(1024)S(1)}, f32[2048]{0:T(1024)}, u32[]{:S(2)}) copy-start(f32[2048]{0:T(1024)} %param.26) | copy-start | bytes 24580
  158.2 14.5 %all-to-all-start.5 = ((bf16[8,128,256]{2,1,0:T(8,128)(2,1)}), bf16[8,128,256]{2,1,0:T(8,128)(2,1)S(1)}, u32[]{:S(2)}, u32[]{:S(2)}) async-start(bf16[8,128,256]{2,1,0:T(8,128)(2,1)} %attend.1), calls=%async_computation.5 | async-start | bytes 1048576 | tf_op jit(solution)/shard_map/all_to_all | solution.py:114
Sparse Core Ops, SparseCore 0:
  27.5 81.4 all-gather.2

commit v2 on v1

v2 whole, which is shorter than its diff:
```python
import functools
import math

import jax
import jax.numpy as jnp
from jax import lax
from jax.experimental import pallas as pl
from jax.experimental.pallas import tpu as pltpu
from jax.sharding import Mesh
from jax.sharding import PartitionSpec as P


MH = 128
P_SIZE = 64
STATE = 128
HD = 128
CONV = 4
SEQ = ("xh", "y", "z")

norm_epsilon = 1e-05
lowest_score = -1e30
EXP2_SCALE = math.log2(math.e) / math.sqrt(HD)


def exchanged(value, axes):
    return lax.all_to_all(value, axes, 0, 0, tiled=True)


def conv_silu(raw_rows, weights, history):
    padded = jnp.concatenate([history, raw_rows], axis=0).astype(jnp.float32)
    length = raw_rows.shape[0]
    summed = jnp.zeros((length, raw_rows.shape[1]), jnp.float32)
    for offset in range(weights.shape[0]):
        summed = summed + weights[offset][None, :] * padded[offset : offset + length]
    return jax.nn.silu(summed)


def attend_kernel(parts, opening, closing, *refs):
    here_ref, q_ref = refs[:2]
    kv_refs = refs[2 : 2 + parts]
    refs = refs[2 + parts :]
    if opening:
        old_m_ref = old_l_ref = old_acc_ref = None
    else:
        old_m_ref, old_l_ref, old_acc_ref = refs[:3]
        refs = refs[3:]
    if closing:
        o_ref, s0_ref, s1_ref, m_ref, l_ref, acc_ref = refs
    else:
        m_ref, l_ref, acc_ref, s0_ref, s1_ref = refs
    sides, length, width = q_ref.shape
    rows = 2 * length
    lanes = 2 * HD
    turns = width // lanes
    zs = kv_refs[0].shape[0]
    span = zs * length
    s_refs = (s0_ref, s1_ref)
    if opening:
        m_ref[...] = jnp.full_like(m_ref, lowest_score)
        l_ref[...] = jnp.zeros_like(l_ref)
        acc_ref[...] = jnp.zeros_like(acc_ref)
    else:
        m_ref[...] = old_m_ref[...]
        l_ref[...] = old_l_ref[...]
        acc_ref[...] = old_acc_ref[...]

    def scores(kv_ref, side, line, turn):
        both = q_ref[side, :, turn * lanes : (turn + 1) * lanes]
        q = jnp.concatenate([both[:, :HD], both[:, HD:]], axis=0)
        k = kv_ref[:, line, :, :HD].reshape(span, HD)
        return lax.dot_general(k, q, (((1,), (1,)), ((), ())), preferred_element_type=jnp.float32)

    def update(kv_ref, side, line, turn, s):
        at = side * turns + turn
        m = m_ref[at]
        new = jnp.maximum(m, jnp.max(s, axis=0, keepdims=True))
        p = jnp.exp2((s - new) * EXP2_SCALE)
        factor = jnp.exp2((m - new) * EXP2_SCALE)
        m_ref[at] = new
        l_ref[at] = l_ref[at] * factor + jnp.sum(p, axis=0, keepdims=True)
        v = jnp.concatenate([kv_ref[z, line, :, HD:] for z in range(zs)], axis=1)
        acc_ref[at] = acc_ref[at] * factor + jnp.dot(
            v, p.astype(jnp.bfloat16), preferred_element_type=jnp.float32
        )

    def whole(kv_ref, count):
        def pick(i):
            i = jnp.minimum(i, count - 1)
            return jnp.where(i == 1, 0, 1), jnp.where(i == 2, 1, 0)

        s_refs[0][...] = scores(kv_ref, 1, 0, 0)

        def one(i, _):
            for turn in range(turns):
                if turn < turns - 1:
                    side, line = pick(i)
                    s_refs[1 - turn % 2][...] = scores(kv_ref, side, line, turn + 1)
                else:
                    side, line = pick(i + 1)
                    s_refs[1 - turn % 2][...] = scores(kv_ref, side, line, 0)
                side, line = pick(i)
                update(kv_ref, side, line, turn, s_refs[turn % 2][...])
            return 0

        lax.fori_loop(0, count, one, 0)

    for k in range(parts):
        if opening:
            kv_ref = kv_refs[k]
            place = lax.broadcasted_iota(jnp.int32, (span, rows), 1) % length
            place = place + here_ref[0] * length
            key_row = lax.broadcasted_iota(jnp.int32, (span, rows), 0)
            key_z = (here_ref[0] + zs - key_row // length) % zs
            allowed = key_z * length + key_row % length <= place
            s_refs[0][...] = scores(kv_ref, 0, 0, 0)

            def diagonal(side, _):
                for turn in range(turns):
                    ahead = side if turn < turns - 1 else jnp.minimum(side + 1, sides - 1)
                    s_refs[1 - turn % 2][...] = scores(kv_ref, ahead, ahead, (turn + 1) % turns)
                    s = jnp.where(allowed, s_refs[turn % 2][...], lowest_score)
                    update(kv_ref, side, side, turn, s)
                return 0

            lax.fori_loop(0, sides, diagonal, 0)
            whole(kv_ref, 1)
        else:
            whole(kv_refs[k], jnp.where(here_ref[2 + k] < here_ref[1], 3, 1))

    if closing:

        def close(side, _):
            for turn in range(turns):
                at = side * turns + turn
                out = acc_ref[at] / l_ref[at]
                for pair in range(2):
                    left = turn * lanes + pair * HD
                    piece = out[:, pair * length : (pair + 1) * length]
                    o_ref[side, :, left : left + HD] = piece.T.astype(jnp.bfloat16)
            return 0

        lax.fori_loop(0, sides, close, 0)


def attend(here, q, kvs, state, closing):
    sides, length, width = q.shape
    parts = len(kvs)
    span = kvs[0].shape[0] * length
    rows = 2 * length
    held = sides * width // (2 * HD)
    pairs = parts * 3 * width // HD * length * span
    vmem = pl.BlockSpec(memory_space=pltpu.VMEM)
    kept = [
        ((held, 1, rows), jnp.float32),
        ((held, 1, rows), jnp.float32),
        ((held, HD, rows), jnp.float32),
    ]
    scratch = [pltpu.VMEM((span, rows), jnp.float32)] * 2
    if closing:
        out_shape = jax.ShapeDtypeStruct((sides, length, width), jnp.bfloat16)
        out_specs = vmem
        scratch = scratch + [pltpu.VMEM(*one) for one in kept]
    else:
        out_shape = [jax.ShapeDtypeStruct(*one) for one in kept]
        out_specs = [vmem] * 3
    return pl.pallas_call(
        functools.partial(attend_kernel, parts, not state, closing),
        out_shape=out_shape,
        in_specs=[pl.BlockSpec(memory_space=pltpu.SMEM)] + [vmem] * (1 + parts + len(state)),
        out_specs=out_specs,
        scratch_shapes=scratch,
        cost_estimate=pl.CostEstimate(
            flops=pairs * HD * 4,
            bytes_accessed=parts * kvs[0].size * 2 + q.size * 4,
            transcendentals=pairs,
        ),
        compiler_params=pltpu.CompilerParams(vmem_limit_bytes=14 * 1024 * 1024),
        name="attend",
    )(here, q, *kvs, *state)


def moved(value, axis, by):
    size = lax.axis_size(axis)
    return lax.ppermute(value, axis, [(i, (i + by) % size) for i in range(size)])


def swapped(mine, others):
    first = lax.axis_index("xh") == 0
    given = moved(others, "xh", 1)
    return jnp.where(first, mine, given), jnp.where(first, given, mine)


def chosen(pair, other):
    first = lax.axis_index("xh") == (1 if other else 0)
    return jnp.where(first, pair[0], pair[1])


def prepare_kernel(here_ref, k_ref, v_ref, x_ref, b_ref, c_ref, kept_ref, given_ref, edge_ref):
    first = here_ref[0] == 0
    k = k_ref[...]
    v = v_ref[...]
    blocks = []
    for head in range(2):
        at = slice(head * HD, (head + 1) * HD)
        blocks.append(jnp.concatenate([k[:, at], v[:, at].T], axis=1))
    kept_ref[...] = jnp.where(first, blocks[0], blocks[1])
    given_ref[...] = jnp.where(first, blocks[1], blocks[0])
    reach = edge_ref.shape[0]
    at = 0
    for ref in (x_ref, b_ref, c_ref):
        edge_ref[:, at : at + ref.shape[1]] = ref[ref.shape[0] - reach :]
        at += ref.shape[1]


def prepare(keys, values, mixer_input, input_matrix, output_matrix):
    length, kv_width = keys.shape
    last = length // 16 - 1
    widths = [mixer_input.shape[1], input_matrix.shape[1], output_matrix.shape[1]]
    here = lax.axis_index("xh").astype(jnp.int32).reshape(1)
    whole = pl.BlockSpec((length, kv_width), lambda i: (0, 0))
    return pl.pallas_call(
        prepare_kernel,
        grid=(1,),
        out_shape=[
            jax.ShapeDtypeStruct((length, 2 * HD), keys.dtype),
            jax.ShapeDtypeStruct((length, 2 * HD), keys.dtype),
            jax.ShapeDtypeStruct((CONV - 1, sum(widths)), mixer_input.dtype),
        ],
        in_specs=[pl.BlockSpec(memory_space=pltpu.SMEM), whole, whole]
        + [pl.BlockSpec((16, width), lambda i: (last, 0)) for width in widths],
        out_specs=[
            pl.BlockSpec((length, 2 * HD), lambda i: (0, 0)),
            pl.BlockSpec((length, 2 * HD), lambda i: (0, 0)),
            pl.BlockSpec((CONV - 1, sum(widths)), lambda i: (0, 0)),
        ],
        cost_estimate=pl.CostEstimate(flops=2000000, bytes_accessed=400000, transcendentals=0),
        name="prepare",
    )(here, keys, values, mixer_input, input_matrix, output_matrix)


def pack_kernel(*refs):
    for k, ref in enumerate(refs[:-1]):
        refs[-1][k] = ref[...]


def packed(blocks):
    vmem = pl.BlockSpec(memory_space=pltpu.VMEM)
    total = len(blocks) * blocks[0].size
    return pl.pallas_call(
        pack_kernel,
        out_shape=jax.ShapeDtypeStruct((len(blocks), *blocks[0].shape), blocks[0].dtype),
        in_specs=[vmem] * len(blocks),
        out_specs=vmem,
        cost_estimate=pl.CostEstimate(flops=total, bytes_accessed=4 * total, transcendentals=0),
        compiler_params=pltpu.CompilerParams(vmem_limit_bytes=4 * 1024 * 1024),
        name="pack",
    )(*blocks)


def gathered_keys(kept, given):
    own = jnp.stack(swapped(kept, given))
    ups, downs = [own], [own]
    far = lax.axis_size("z") // 2
    for step in range(1, far + 1):
        ups.append(moved(ups[-1], "z", 1))
        if step < far:
            downs.append(moved(downs[-1], "z", -1))
    return packed(ups + downs[:0:-1])


def carry_kernel(piece_ref, o_ref):
    count, rows = o_ref.shape[0], o_ref.shape[1]

    def step(j, state):
        o_ref[j] = state.astype(jnp.bfloat16)
        block = piece_ref[j].astype(jnp.float32)
        log = block[rows : rows + 1] + block[rows + 1 : rows + 2] + block[rows + 2 : rows + 3]
        return jnp.exp(log) * state + block[:rows]

    lax.fori_loop(0, count, step, jnp.zeros((rows, STATE), jnp.float32), unroll=8)


def carry_states(pieces):
    count, rows = pieces.shape[0], pieces.shape[1] - 8
    return pl.pallas_call(
        carry_kernel,
        out_shape=jax.ShapeDtypeStruct((count, rows, STATE), jnp.bfloat16),
        in_specs=[pl.BlockSpec(memory_space=pltpu.VMEM)],
        out_specs=pl.BlockSpec(memory_space=pltpu.VMEM),
        cost_estimate=pl.CostEstimate(
            flops=1000000, bytes_accessed=pieces.size * 4, transcendentals=count * 128
        ),
        compiler_params=pltpu.CompilerParams(vmem_limit_bytes=4 * 1024 * 1024),
        name="carry_states",
    )(pieces)


def entering_state(own, log_total, first, second):
    heads = own.shape[0]
    count = lax.axis_size(SEQ)
    rows = heads * P_SIZE // count
    per_head = count // heads
    body = own.astype(jnp.bfloat16).reshape(count, rows, STATE)
    log = jnp.repeat(log_total, per_head)[:, None, None]
    high = log.astype(jnp.bfloat16)
    rest = log - high.astype(jnp.float32)
    mid = rest.astype(jnp.bfloat16)
    low = (rest - mid.astype(jnp.float32)).astype(jnp.bfloat16)
    which = lax.broadcasted_iota(jnp.int32, (count, 8, STATE), 1)
    zero = jnp.zeros((), jnp.bfloat16)
    tail = jnp.where(which == 0, high, jnp.where(which == 1, mid, jnp.where(which == 2, low, zero)))
    pieces = jnp.concatenate([body, tail], axis=1)
    pieces = exchanged(pieces, SEQ)
    pieces, first = lax.optimization_barrier((pieces, first))
    entering = carry_states(pieces)
    entering = exchanged(entering, SEQ)
    entering, state = lax.optimization_barrier((entering, second(first)))
    return entering.reshape(heads, P_SIZE, STATE), state


def summed_over_tp(value):
    value = value[None]
    others = [
        lax.ppermute(value, "tp", [(i, i ^ by) for i in range(lax.axis_size("tp"))])
        for by in range(1, lax.axis_size("tp"))
    ]
    return (value + others[0] + others[1] + others[2])[0]


def mixer_local(
    mixer_input,
    gate_input,
    input_matrix,
    output_matrix,
    step_raw,
    step_bias,
    decay_rate,
    skip_weight,
    conv_mixer,
    conv_input,
    conv_output,
    norm_gain,
    edge,
    first,
    second,
):
    length, width = mixer_input.shape
    heads = width // P_SIZE
    groups = input_matrix.shape[1] // STATE
    shared = heads // groups
    count = lax.axis_size(SEQ)
    edge = lax.ppermute(edge, SEQ, [(i, i + 1) for i in range(count - 1)])
    mid = width + input_matrix.shape[1]
    signal = conv_silu(mixer_input, conv_mixer, edge[:, :width]).reshape(length, heads, P_SIZE)
    b_state = conv_silu(input_matrix, conv_input, edge[:, width:mid])
    c_state = conv_silu(output_matrix, conv_output, edge[:, mid:])
    b_state = b_state.reshape(length, groups, STATE)
    c_state = c_state.reshape(length, groups, STATE)
    step_size = jax.nn.softplus(step_raw + step_bias[None, :])
    places = jnp.arange(length, dtype=jnp.int32)
    causal = places[:, None] >= places[None, :]
    log_decay = jnp.cumsum(-step_size * decay_rate[None, :], axis=0)
    by_head = log_decay.T
    spread = jnp.where(causal, by_head[:, :, None] - by_head[:, None, :], 0.0)
    decays = jnp.where(causal, jnp.exp(spread), 0.0)
    coupling = jnp.einsum("tgn,sgn->gts", c_state, b_state)
    mixing = decays * jnp.repeat(coupling, shared, axis=0)
    scaled = signal * step_size[:, :, None]
    closing = jnp.exp(log_decay[-1][None, :] - log_decay)
    weighted = (scaled * closing[:, :, None]).reshape(length, groups, shared * P_SIZE)
    own = jnp.einsum("sgq,sgn->gqn", weighted, b_state).reshape(heads, P_SIZE, STATE)
    entering, first = entering_state(own, log_decay[-1], first, second)
    output = jnp.einsum("hts,shp->thp", mixing, scaled)
    later = jnp.einsum(
        "tgn,gqn->tgq",
        c_state.astype(jnp.bfloat16),
        entering.reshape(groups, shared * P_SIZE, STATE),
        preferred_element_type=jnp.float32,
    ).reshape(length, heads, P_SIZE)
    mixed = output + jnp.exp(log_decay)[:, :, None] * later
    mixed = mixed + skip_weight[None, :, None] * signal
    gated = mixed.reshape(length, width) * jax.nn.silu(gate_input.astype(jnp.float32))
    partial = jnp.sum(gated * gated, axis=1)
    squares = summed_over_tp(partial)
    scaling = lax.rsqrt(squares / (MH * P_SIZE) + norm_epsilon)
    return (gated * scaling[:, None] * norm_gain[None, :]).astype(jnp.bfloat16), first


def shards(
    mixer_input,
    gate_input,
    input_matrix,
    output_matrix,
    step_raw,
    step_bias,
    decay_rate,
    skip_weight,
    conv_mixer,
    conv_input,
    conv_output,
    norm_gain,
    queries,
    keys,
    values,
):
    half = queries.shape[1] // 2
    halves = (queries[:, :half], queries[:, half:])
    q = jnp.stack(swapped(chosen(halves, False), chosen(halves, True)))
    kept, given, edge = prepare(keys, values, mixer_input, input_matrix, output_matrix)
    kv = gathered_keys(kept, given)
    above = moved(kv, "y", 1)
    below = moved(kv, "y", -1)
    near = kv.shape[0] // 2
    far_low = moved(above[:near], "y", 1)
    far_high = moved(below[near:], "y", -1)
    y, ys = lax.axis_index("y"), lax.axis_size("y")
    z = lax.axis_index("z")

    def here(*ups):
        return jnp.stack([z, y] + [(y + up) % ys for up in ups]).astype(jnp.int32)

    state = attend(here(0), q, [kv], [], False)
    mixer_out, state = mixer_local(
        mixer_input,
        gate_input,
        input_matrix,
        output_matrix,
        step_raw,
        step_bias,
        decay_rate,
        skip_weight,
        conv_mixer,
        conv_input,
        conv_output,
        norm_gain,
        edge,
        state,
        lambda state: attend(here(ys - 1, 1), q, [above, below], state, False),
    )
    far = jnp.concatenate([far_low, far_high], axis=0)
    out = attend(here(2), q, [far], state, True)
    halves = swapped(chosen(out, False), chosen(out, True))
    attention_out = jnp.concatenate(halves, axis=1)
    return (mixer_out, attention_out)


def solution(mesh):
    torus = Mesh(mesh.devices.reshape(2, 4, 8, mesh.shape["tp"]), ("xh", "y", "z", "tp"))
    placed = (
        P(SEQ, "tp"),
        P(SEQ, "tp"),
        P(SEQ, "tp"),
        P(SEQ, "tp"),
        P(SEQ, "tp"),
        P("tp"),
        P("tp"),
        P("tp"),
        P(None, "tp"),
        P(None, "tp"),
        P(None, "tp"),
        P("tp"),
        P(SEQ, "tp"),
        P(SEQ, "tp"),
        P(SEQ, "tp"),
    )

    return jax.shard_map(
        shards, mesh=torus, in_specs=placed, out_specs=(P(SEQ, "tp"), P(SEQ, "tp")), check_vma=False
    )
```

time: 182 us -> 130 us (0.71)
  the two profiles are of different devices: /device:TPU:1 before, /device:TPU:30 now
where the time goes in v2:
time: 130 us; the launch traced here: 129 us
  starting transfers between devices  48 us (37%)
  waiting for transfers between devices  30.2 us (23%)
  Pallas kernels  26.8 us (21%)
  other arithmetic  10.4 us (8%)
  local copies, waits for them, and re-layouts  8.81 us (7%)
  matrix products  3.8 us (3%)
    ppermute x14, waiting for transfers between devices, moved(): lax.ppermute(value, axis, [(i, (i + by) % size) for i in range(size)])  28.9 us
    all_to_all x2, starting transfers between devices, exchanged(): return lax.all_to_all(value, axes, 0, 0, tiled=True)  26.1 us
    pallas_call x3, Pallas kernels, attend(): pl.pallas_call(functools.partial(attend_kernel, parts, not state, closing...  24 us
    ppermute x14, starting transfers between devices, moved(): lax.ppermute(value, axis, [(i, (i + by) % size) for i in range(size)])  16 us
    unnamed x38, local copies, waits for them, and re-layouts  4.16 us
    ppermute x1, starting transfers between devices, mixer_local(): edge = lax.ppermute(edge, SEQ, [(i, i + 1) for i in range(count - 1)])  3.81 us
    dot_general x1, matrix products, mixer_local(): output = jnp.einsum('hts,shp->thp', mixing, scaled)  3.08 us
  transfers between devices with their start and end apart: 20, of which 6 were waited for; matrix products, arithmetic and copies ran while one was open for 10% of the time, Pallas kernels for 19%

profile of v2, /device:TPU:30, one launch (start us, length us, event | category | flops | bytes accessed | tf_op | source)
XLA Modules:
  0.0 129.2 jit_solution(11189560216838031008)
XLA Ops:
  0.7 1.7 %prepare.1 = (bf16[128,256]{1,0:T(8,128)(2,1)}, bf16[128,256]{1,0:T(8,128)(2,1)}, bf16[3,2560]{1,0:T(4,128)(2,1)}) custom-call(s32[1]{0:T(128)} %bitcast.1.here_ref, bf16[128,256]{1,0:T(8,128)(2,1)} %k_ref.1, bf16[128,256]{1,0:T(8,128)(2,1)} %v_ref.1, bf16[128,2048]{1,0:T(8,128)(2,1)} %x_ref.1, bf16[128,256]{1,0:T(8,128)(2,1)} %b_ref.1, bf16[128,256]{1,0:T(8,128)(2,1)} %c_ref.1), custom_call_target="tpu_custom_call" | custom-call | flops 2000000 | bytes 400000 | tf_op jit(solution)/shard_map/prepare/pallas_call | solution.py:221
  2.4 3.8 %collective-permute-start = (bf16[3,2560]{1,0:T(4,128)(2,1)}, bf16[3,2560]{1,0:T(4,128)(2,1)S(1)}, u32[]{:S(2)}, u32[]{:S(2)}) collective-permute-start(bf16[3,2560]{1,0:T(4,128)(2,1)} %get-tuple-element.19), channel_id=1, source_target_pairs={{0,4},{4,8},{8,12},{12,16},{16,20},{20,24},{24,28},{28,32},{32,36}... | collective-permute-start | bytes 46088 | tf_op jit(solution)/shard_map/ppermute | solution.py:352
  6.2 1.5 %collective-permute-start.2 = (bf16[128,256]{1,0:T(8,128)(2,1)}, bf16[128,256]{1,0:T(8,128)(2,1)S(1)}, u32[]{:S(2)}, u32[]{:S(2)}) collective-permute-start(bf16[128,256]{1,0:T(8,128)(2,1)} %get-tuple-element.21), channel_id=1, source_target_pairs={{0,128},{128,0},{1,129},{129,1},{2,130},{130,2},{3,131},{131,3},{4... | collective-permute-start | bytes 196616 | tf_op jit(solution)/shard_map/ppermute | solution.py:184
  8.6 0.9 fusion.27
  10.9 1.3 %collective-permute-done = bf16[3,2560]{1,0:T(4,128)(2,1)S(1)} collective-permute-done((bf16[3,2560]{1,0:T(4,128)(2,1)}, bf16[3,2560]{1,0:T(4,128)(2,1)S(1)}, u32[]{:S(2)}, u32[]{:S(2)}) %collective-permute-start) | collective-permute-done | bytes 15392 | tf_op jit(solution)/shard_map/ppermute | solution.py:352
  16.3 2.7 %collective-permute-start.7 = (bf16[2,128,256]{2,1,0:T(8,128)(2,1)S(1)}, bf16[2,128,256]{2,1,0:T(8,128)(2,1)S(1)}, u32[]{:S(2)}, u32[]{:S(2)}) collective-permute-start(bf16[2,128,256]{2,1,0:T(8,128)(2,1)S(1)} %pad_maximum_fusion.4.refs_0_), channel_id=1, source_target_pairs={{0,28},{4,0},{8,4},{12,8},{16,12},{20,16},{24,20},{28,24},{1,29},{... | collective-permute-start | bytes 393224 | tf_op jit(solution)/shard_map/ppermute | solution.py:184
  19.0 2.6 %collective-permute-done.3.refs_1_ = bf16[2,128,256]{2,1,0:T(8,128)(2,1)S(1)} collective-permute-done((bf16[2,128,256]{2,1,0:T(8,128)(2,1)S(1)}, bf16[2,128,256]{2,1,0:T(8,128)(2,1)S(1)}, u32[]{:S(2)}, u32[]{:S(2)}) %collective-permute-start.3) | collective-permute-done | bytes 131104 | tf_op jit(solution)/shard_map/ppermute | solution.py:184
  22.4 13.0 %all-to-all-start = ((bf16[64,40,128]{2,1,0:T(8,128)(2,1)}), bf16[64,40,128]{2,1,0:T(8,128)(2,1)S(1)}, u32[]{:S(2)}, u32[]{:S(2)}) async-start(bf16[64,40,128]{2,1,0:T(8,128)(2,1)} %pad_maximum_fusion.1), calls=%async_computation | async-start | bytes 1310720 | tf_op jit(solution)/shard_map/all_to_all | solution.py:26
  35.5 2.8 %collective-permute-start.8 = (bf16[2,128,256]{2,1,0:T(8,128)(2,1)S(1)}, bf16[2,128,256]{2,1,0:T(8,128)(2,1)S(1)}, u32[]{:S(2)}, u32[]{:S(2)}) collective-permute-start(bf16[2,128,256]{2,1,0:T(8,128)(2,1)S(1)} %collective-permute-done.7.refs_7_), channel_id=1, source_target_pairs={{0,28},{4,0},{8,4},{12,8},{16,12},{20,16},{24,20},{28,24},{1,29},{... | collective-permute-start | bytes 393224 | tf_op jit(solution)/shard_map/ppermute | solution.py:184
  39.4 12.4 %collective-permute-done.8.refs_6_ = bf16[2,128,256]{2,1,0:T(8,128)(2,1)S(1)} collective-permute-done((bf16[2,128,256]{2,1,0:T(8,128)(2,1)S(1)}, bf16[2,128,256]{2,1,0:T(8,128)(2,1)S(1)}, u32[]{:S(2)}, u32[]{:S(2)}) %collective-permute-start.8) | collective-permute-done | bytes 131104 | tf_op jit(solution)/shard_map/ppermute | solution.py:184
  51.8 1.7 %collective-permute-start.9 = (bf16[2,128,256]{2,1,0:T(8,128)(2,1)S(1)}, bf16[2,128,256]{2,1,0:T(8,128)(2,1)S(1)}, u32[]{:S(2)}, u32[]{:S(2)}) collective-permute-start(bf16[2,128,256]{2,1,0:T(8,128)(2,1)S(1)} %collective-permute-done.8.refs_6_), channel_id=1, source_target_pairs={{0,28},{4,0},{8,4},{12,8},{16,12},{20,16},{24,20},{28,24},{1,29},{... | collective-permute-start | bytes 393224 | tf_op jit(solution)/shard_map/ppermute | solution.py:184
  53.9 2.9 %collective-permute-done.9.refs_5_ = bf16[2,128,256]{2,1,0:T(8,128)(2,1)S(1)} collective-permute-done((bf16[2,128,256]{2,1,0:T(8,128)(2,1)S(1)}, bf16[2,128,256]{2,1,0:T(8,128)(2,1)S(1)}, u32[]{:S(2)}, u32[]{:S(2)}) %collective-permute-start.9) | collective-permute-done | bytes 131104 | tf_op jit(solution)/shard_map/ppermute | solution.py:184
  56.8 2.9 %collective-permute-done.6.refs_4_ = bf16[2,128,256]{2,1,0:T(8,128)(2,1)S(1)} collective-permute-done((bf16[2,128,256]{2,1,0:T(8,128)(2,1)S(1)}, bf16[2,128,256]{2,1,0:T(8,128)(2,1)S(1)}, u32[]{:S(2)}, u32[]{:S(2)}) %collective-permute-start.6) | collective-permute-done | bytes 131104 | tf_op jit(solution)/shard_map/ppermute | solution.py:184
  60.2 1.6 %collective-permute-start.11 = (bf16[8,2,128,256]{3,2,1,0:T(8,128)(2,1)S(1)}, bf16[8,2,128,256]{3,2,1,0:T(8,128)(2,1)}, u32[]{:S(2)}, u32[]{:S(2)}) collective-permute-start(bf16[8,2,128,256]{3,2,1,0:T(8,128)(2,1)S(1)} %pack.1.refs_2_), channel_id=1, source_target_pairs={{0,96},{32,0},{64,32},{96,64},{1,97},{33,1},{65,33},{97,65},{2,98}... | collective-permute-start | bytes 3145736 | tf_op jit(solution)/shard_map/ppermute | solution.py:184
  61.9 1.2 select_bitcast_fusion.2
  63.1 6.4 %attend.3 = (f32[8,1,256]{2,1,0:T(1,128)S(1)}, f32[8,1,256]{2,1,0:T(1,128)S(1)}, f32[8,128,256]{2,1,0:T(8,128)S(1)}) custom-call(s32[3]{0:T(128)S(1)} %pad_add_fusion.refs_0_, bf16[2,128,1024]{2,1,0:T(8,128)(2,1)S(1)} %pad_maximum_fusion.2.refs_1_, bf16[8,2,128,256]{3,2,1,0:T(8,128)(2,1)S(1)} %pack.1.refs_2_), custom_call_target="tpu_custom_call" | custom-call | flops 1610612736 | bytes 2097152 | tf_op jit(solution)/shard_map/attend/pallas_call | solution.py:166
  69.5 1.0 copy-done.2
  70.4 1.0 carry_states.1
  71.5 13.0 %all-to-all-start.1 = ((bf16[64,32,128]{2,1,0:T(8,128)(2,1)}), bf16[64,32,128]{2,1,0:T(8,128)(2,1)S(1)}, u32[]{:S(2)}, u32[]{:S(2)}) async-start(bf16[64,32,128]{2,1,0:T(8,128)(2,1)} %carry_states.1), calls=%async_computation.1 | async-start | bytes 1048576 | tf_op jit(solution)/shard_map/all_to_all | solution.py:26
  84.9 1.1 slice.156
  86.0 0.9 collective-permute-start.16
  87.0 2.5 %collective-permute-start.15 = (bf16[4,2,128,256]{3,2,1,0:T(8,128)(2,1)S(1)}, bf16[4,2,128,256]{3,2,1,0:T(8,128)(2,1)S(1)}, u32[]{:S(2)}, u32[]{:S(2)}) collective-permute-start(bf16[4,2,128,256]{3,2,1,0:T(8,128)(2,1)S(1)} %slice.155), channel_id=1, source_target_pairs={{0,32},{32,64},{64,96},{96,0},{1,33},{33,65},{65,97},{97,1},{2,34}... | collective-permute-start | bytes 1572872 | tf_op jit(solution)/shard_map/ppermute | solution.py:184
  89.6 1.5 %bitcast_multiply_fusion = bf16[32,128,128]{2,1,0:T(8,128)(2,1)} fusion(f32[2,128,128]{2,1,0:T(8,128)S(1)} %fusion.12, f32[32,128]{1,0:T(8,128)S(1)} %copy.31, pred[128,128]{1,0:T(8,128)(4,1)S(1)} %iota_compare_fusion), kind=kLoop, calls=%fused_computation | loop fusion | flops 2621440 | bytes 1212416 | tf_op jit(solution)/shard_map/mul | solution.py:367
  91.2 11.1 %attend.4 = (f32[8,1,256]{2,1,0:T(1,128)S(1)}, f32[8,1,256]{2,1,0:T(1,128)S(1)}, f32[8,128,256]{2,1,0:T(8,128)S(1)}) custom-call(s32[4]{0:T(128)S(1)} %pad_add_fusion.2.refs_0_, bf16[2,128,1024]{2,1,0:T(8,128)(2,1)S(1)} %pad_maximum_fusion.2.refs_1_, bf16[8,2,128,256]{3,2,1,0:T(8,128)(2,1)S(1)} %collective-permute-done.10.refs_2_, ...), custom_call_target="tpu_custom_call" | custom-call | flops 3221225472 | bytes 3145728 | tf_op jit(solution)/shard_map/attend/pallas_call | solution.py:166
  102.3 1.0 copy-done
  103.7 0.9 copy-done.5
  104.6 3.1 %fusion.1 = f32[128,32,64]{0,2,1:T(8,128)} fusion(bf16[32,128,128]{2,1,0:T(8,128)(2,1)} %bitcast_multiply_fusion, f32[128,32,64]{0,2,1:T(8,128)S(1)} %bitcast.81, f32[128,32,64]{0,2,1:T(8,128)S(1)} %bitcast.82, f32[32]{0:T(128)S(1)} %copy-done.18, f32[128,32]{0,1:T(8,128)S(1)} %copy.35, f32[128,32]{0,1:T(8,128)S(1)} %get-tuple-element.37), kind=kOutput, calls=%fused_computation.3 | convolution fusion | flops 68419584 | bytes 4227200 | tf_op jit(solution)/shard_map/hts,shp->thp/dot_general | solution.py:373
  107.7 1.6 %copy.40 = f32[128,2048]{1,0:T(8,128)S(1)} copy(f32[128,2048]{0,1:T(8,128)} %bitcast.83) | data formatting | bytes 2097152 | tf_op jit(solution)/shard_map/reshape | solution.py:382
  110.2 1.7 %collective-permute-start.12 = (f32[1,128]{1,0:T(1,128)S(1)}, f32[1,128]{1,0:T(1,128)S(1)}, u32[]{:S(2)}, u32[]{:S(2)}) collective-permute-start(f32[1,128]{1,0:T(1,128)S(1)} %bitcast.103), channel_id=1, source_target_pairs={{0,1},{1,0},{2,3},{3,2},{4,5},{5,4},{6,7},{7,6},{8,9},{9,8},{10,11... | collective-permute-start | bytes 1544 | tf_op jit(solution)/shard_map/ppermute | solution.py:324
  112.0 6.5 %attend.5 = bf16[2,128,1024]{2,1,0:T(8,128)(2,1)S(1)} custom-call(s32[3]{0:T(128)S(1)} %pad_add_fusion.3.refs_0_, bf16[2,128,1024]{2,1,0:T(8,128)(2,1)S(1)} %pad_maximum_fusion.2.refs_1_, bf16[8,2,128,256]{3,2,1,0:T(8,128)(2,1)S(1)} %pad_maximum_fusion.refs_2_, f32[8,1,256]{2,1,0:T(1,128)S(1)} %get-tuple-element.33.refs_3_, ...), custom_call_target="tpu_custom_call" | custom-call | flops 1610612736 | bytes 2097152 | tf_op jit(solution)/shard_map/attend/pallas_call | solution.py:166
  119.0 1.2 multiply_convert_fusion
  120.2 8.2 %collective-permute-done.17 = bf16[128,1024]{1,0:T(8,128)(2,1)S(1)} collective-permute-done((bf16[128,1024]{1,0:T(8,128)(2,1)S(1)}, bf16[128,1024]{1,0:T(8,128)(2,1)S(1)}, u32[]{:S(2)}, u32[]{:S(2)}) %collective-permute-start.17) | collective-permute-done | bytes 262176 | tf_op jit(solution)/shard_map/ppermute | solution.py:184
  (105 shorter events, 12.4 us)
Async XLA Ops:
  0.6 11.6 %copy-start.6 = (bf16[128,2048]{1,0:T(8,128)(2,1)S(1)}, bf16[128,2048]{1,0:T(8,128)(2,1)}, u32[]{:S(2)}) copy-start(bf16[128,2048]{1,0:T(8,128)(2,1)} %x_ref.1) | copy-start | bytes 1572868
  0.6 10.2 %copy-start.16 = (f32[4,256]{1,0:T(4,128)S(1)}, f32[4,256]{1,0:T(4,128)}, u32[]{:S(2)}) copy-start(f32[4,256]{1,0:T(4,128)} %param.24) | copy-start | bytes 12292
  2.4 9.9 %collective-permute-start = (bf16[3,2560]{1,0:T(4,128)(2,1)}, bf16[3,2560]{1,0:T(4,128)(2,1)S(1)}, u32[]{:S(2)}, u32[]{:S(2)}) collective-permute-start(bf16[3,2560]{1,0:T(4,128)(2,1)} %get-tuple-element.19), channel_id=1, source_target_pairs={{0,4},{4,8},{8,12},{12,16},{16,20},{20,24},{24,28},{28,32},{32,36}... | collective-permute-start | bytes 46088 | tf_op jit(solution)/shard_map/ppermute | solution.py:352
  6.2 8.6 %collective-permute-start.2 = (bf16[128,256]{1,0:T(8,128)(2,1)}, bf16[128,256]{1,0:T(8,128)(2,1)S(1)}, u32[]{:S(2)}, u32[]{:S(2)}) collective-permute-start(bf16[128,256]{1,0:T(8,128)(2,1)} %get-tuple-element.21), channel_id=1, source_target_pairs={{0,128},{128,0},{1,129},{129,1},{2,130},{130,2},{3,131},{131,3},{4... | collective-permute-start | bytes 196616 | tf_op jit(solution)/shard_map/ppermute | solution.py:184
  14.8 6.8 %copy-start.9 = (bf16[16,2,8,128]{3,2,1,0:T(8,128)(2,1)}, bf16[16,2,8,128]{3,2,1,0:T(8,128)(2,1)S(1)}, u32[]{:S(2)}) copy-start(bf16[16,2,8,128]{3,2,1,0:T(8,128)(2,1)S(1)} %multiply_bitcast_fusion) | copy-start | bytes 196612
  15.3 6.3 %collective-permute-start.3 = (bf16[2,128,256]{2,1,0:T(8,128)(2,1)S(1)}, bf16[2,128,256]{2,1,0:T(8,128)(2,1)S(1)}, u32[]{:S(2)}, u32[]{:S(2)}) collective-permute-start(bf16[2,128,256]{2,1,0:T(8,128)(2,1)S(1)} %pad_maximum_fusion.4.refs_0_), channel_id=1, source_target_pairs={{0,4},{4,8},{8,12},{12,16},{16,20},{20,24},{24,28},{28,0},{1,5},{5... | collective-permute-start | bytes 393224 | tf_op jit(solution)/shard_map/ppermute | solution.py:184
  16.3 19.2 %collective-permute-start.7 = (bf16[2,128,256]{2,1,0:T(8,128)(2,1)S(1)}, bf16[2,128,256]{2,1,0:T(8,128)(2,1)S(1)}, u32[]{:S(2)}, u32[]{:S(2)}) collective-permute-start(bf16[2,128,256]{2,1,0:T(8,128)(2,1)S(1)} %pad_maximum_fusion.4.refs_0_), channel_id=1, source_target_pairs={{0,28},{4,0},{8,4},{12,8},{16,12},{20,16},{24,20},{28,24},{1,29},{... | collective-permute-start | bytes 393224 | tf_op jit(solution)/shard_map/ppermute | solution.py:184
  21.6 16.7 %collective-permute-start.4 = (bf16[2,128,256]{2,1,0:T(8,128)(2,1)S(1)}, bf16[2,128,256]{2,1,0:T(8,128)(2,1)S(1)}, u32[]{:S(2)}, u32[]{:S(2)}) collective-permute-start(bf16[2,128,256]{2,1,0:T(8,128)(2,1)S(1)} %collective-permute-done.3.refs_1_), channel_id=1, source_target_pairs={{0,4},{4,8},{8,12},{12,16},{16,20},{20,24},{24,28},{28,0},{1,5},{5... | collective-permute-start | bytes 393224 | tf_op jit(solution)/shard_map/ppermute | solution.py:184
  21.6 16.7 %copy-start.7 = (bf16[128,2048]{1,0:T(8,128)(2,1)S(1)}, bf16[128,2048]{1,0:T(8,128)(2,1)}, u32[]{:S(2)}) copy-start(bf16[128,2048]{1,0:T(8,128)(2,1)} %param.27) | copy-start | bytes 1572868
  22.4 31.4 %copy-start.17 = (f32[4,256]{1,0:T(4,128)S(1)}, f32[4,256]{1,0:T(4,128)}, u32[]{:S(2)}) copy-start(f32[4,256]{1,0:T(4,128)} %param.25) | copy-start | bytes 12292
  22.4 48.0 %all-to-all-start = ((bf16[64,40,128]{2,1,0:T(8,128)(2,1)}), bf16[64,40,128]{2,1,0:T(8,128)(2,1)S(1)}, u32[]{:S(2)}, u32[]{:S(2)}) async-start(bf16[64,40,128]{2,1,0:T(8,128)(2,1)} %pad_maximum_fusion.1), calls=%async_computation | async-start | bytes 1310720 | tf_op jit(solution)/shard_map/all_to_all | solution.py:26
  35.5 16.3 %collective-permute-start.8 = (bf16[2,128,256]{2,1,0:T(8,128)(2,1)S(1)}, bf16[2,128,256]{2,1,0:T(8,128)(2,1)S(1)}, u32[]{:S(2)}, u32[]{:S(2)}) collective-permute-start(bf16[2,128,256]{2,1,0:T(8,128)(2,1)S(1)} %collective-permute-done.7.refs_7_), channel_id=1, source_target_pairs={{0,28},{4,0},{8,4},{12,8},{16,12},{20,16},{24,20},{28,24},{1,29},{... | collective-permute-start | bytes 393224 | tf_op jit(solution)/shard_map/ppermute | solution.py:184
  38.3 15.1 %collective-permute-start.5 = (bf16[2,128,256]{2,1,0:T(8,128)(2,1)S(1)}, bf16[2,128,256]{2,1,0:T(8,128)(2,1)S(1)}, u32[]{:S(2)}, u32[]{:S(2)}) collective-permute-start(bf16[2,128,256]{2,1,0:T(8,128)(2,1)S(1)} %collective-permute-done.4.refs_2_), channel_id=1, source_target_pairs={{0,4},{4,8},{8,12},{12,16},{16,20},{20,24},{24,28},{28,0},{1,5},{5... | collective-permute-start | bytes 393224 | tf_op jit(solution)/shard_map/ppermute | solution.py:184
  39.0 22.8 %collective-permute-start.1 = (bf16[128,1024]{1,0:T(8,128)(2,1)}, bf16[128,1024]{1,0:T(8,128)(2,1)}, u32[]{:S(2)}, u32[]{:S(2)}) collective-permute-start(bf16[128,1024]{1,0:T(8,128)(2,1)} %broadcast_select_fusion.1), channel_id=1, source_target_pairs={{0,128},{128,0},{1,129},{129,1},{2,130},{130,2},{3,131},{131,3},{4... | collective-permute-start | bytes 786440 | tf_op jit(solution)/shard_map/ppermute | solution.py:184
  51.8 5.0 %collective-permute-start.9 = (bf16[2,128,256]{2,1,0:T(8,128)(2,1)S(1)}, bf16[2,128,256]{2,1,0:T(8,128)(2,1)S(1)}, u32[]{:S(2)}, u32[]{:S(2)}) collective-permute-start(bf16[2,128,256]{2,1,0:T(8,128)(2,1)S(1)} %collective-permute-done.8.refs_6_), channel_id=1, source_target_pairs={{0,28},{4,0},{8,4},{12,8},{16,12},{20,16},{24,20},{28,24},{1,29},{... | collective-permute-start | bytes 393224 | tf_op jit(solution)/shard_map/ppermute | solution.py:184
  53.4 6.2 %collective-permute-start.6 = (bf16[2,128,256]{2,1,0:T(8,128)(2,1)S(1)}, bf16[2,128,256]{2,1,0:T(8,128)(2,1)S(1)}, u32[]{:S(2)}, u32[]{:S(2)}) collective-permute-start(bf16[2,128,256]{2,1,0:T(8,128)(2,1)S(1)} %collective-permute-done.5.refs_3_), channel_id=1, source_target_pairs={{0,4},{4,8},{8,12},{12,16},{16,20},{20,24},{24,28},{28,0},{1,5},{5... | collective-permute-start | bytes 393224 | tf_op jit(solution)/shard_map/ppermute | solution.py:184
  59.7 27.2 %collective-permute-start.10 = (bf16[8,2,128,256]{3,2,1,0:T(8,128)(2,1)S(1)}, bf16[8,2,128,256]{3,2,1,0:T(8,128)(2,1)S(1)}, u32[]{:S(2)}, u32[]{:S(2)}) collective-permute-start(bf16[8,2,128,256]{3,2,1,0:T(8,128)(2,1)S(1)} %pack.1.refs_2_), channel_id=1, source_target_pairs={{0,32},{32,64},{64,96},{96,0},{1,33},{33,65},{65,97},{97,1},{2,34}... | collective-permute-start | bytes 3145736 | tf_op jit(solution)/shard_map/ppermute | solution.py:184
  60.2 24.7 %collective-permute-start.11 = (bf16[8,2,128,256]{3,2,1,0:T(8,128)(2,1)S(1)}, bf16[8,2,128,256]{3,2,1,0:T(8,128)(2,1)}, u32[]{:S(2)}, u32[]{:S(2)}) collective-permute-start(bf16[8,2,128,256]{3,2,1,0:T(8,128)(2,1)S(1)} %pack.1.refs_2_), channel_id=1, source_target_pairs={{0,96},{32,0},{64,32},{96,64},{1,97},{33,1},{65,33},{97,65},{2,98}... | collective-permute-start | bytes 3145736 | tf_op jit(solution)/shard_map/ppermute | solution.py:184
  71.5 13.2 %copy-start.11 = (f32[128,32]{1,0:T(8,128)S(1)}, f32[128,32]{1,0:T(8,128)}, u32[]{:S(2)}) copy-start(f32[128,32]{1,0:T(8,128)} %get-tuple-element.44) | copy-start | bytes 49156
  71.5 32.0 %all-to-all-start.1 = ((bf16[64,32,128]{2,1,0:T(8,128)(2,1)}), bf16[64,32,128]{2,1,0:T(8,128)(2,1)S(1)}, u32[]{:S(2)}, u32[]{:S(2)}) async-start(bf16[64,32,128]{2,1,0:T(8,128)(2,1)} %carry_states.1), calls=%async_computation.1 | async-start | bytes 1048576 | tf_op jit(solution)/shard_map/all_to_all | solution.py:26
  84.9 4.6 %copy-start.10 = (bf16[16,2,8,128]{3,2,1,0:T(8,128)(2,1)S(1)}, bf16[16,2,8,128]{3,2,1,0:T(8,128)(2,1)}, u32[]{:S(2)}) copy-start(bf16[16,2,8,128]{3,2,1,0:T(8,128)(2,1)} %copy-done.9) | copy-start | bytes 196612
  86.0 5.1 %copy-start.3 = (f32[8,128,256]{2,1,0:T(8,128)S(1)}, f32[8,128,256]{2,1,0:T(8,128)}, u32[]{:S(2)}) copy-start(f32[8,128,256]{2,1,0:T(8,128)} %copy-done.2) | copy-start | bytes 3145732
  86.0 17.3 %collective-permute-start.16 = (bf16[4,2,128,256]{3,2,1,0:T(8,128)(2,1)S(1)}, bf16[4,2,128,256]{3,2,1,0:T(8,128)(2,1)S(1)}, u32[]{:S(2)}, u32[]{:S(2)}) collective-permute-start(bf16[4,2,128,256]{3,2,1,0:T(8,128)(2,1)S(1)} %slice.156), channel_id=1, source_target_pairs={{0,96},{32,0},{64,32},{96,64},{1,97},{33,1},{65,33},{97,65},{2,98}... | collective-permute-start | bytes 1572872 | tf_op jit(solution)/shard_map/ppermute | solution.py:184
  87.0 16.4 %collective-permute-start.15 = (bf16[4,2,128,256]{3,2,1,0:T(8,128)(2,1)S(1)}, bf16[4,2,128,256]{3,2,1,0:T(8,128)(2,1)S(1)}, u32[]{:S(2)}, u32[]{:S(2)}) collective-permute-start(bf16[4,2,128,256]{3,2,1,0:T(8,128)(2,1)S(1)} %slice.155), channel_id=1, source_target_pairs={{0,32},{32,64},{64,96},{96,0},{1,33},{33,65},{65,97},{97,1},{2,34}... | collective-permute-start | bytes 1572872 | tf_op jit(solution)/shard_map/ppermute | solution.py:184
  103.4 1.2 copy-start.5
  107.7 1.6 %copy-start.8 = (bf16[128,2048]{1,0:T(8,128)(2,1)S(1)}, bf16[128,2048]{1,0:T(8,128)(2,1)}, u32[]{:S(2)}) copy-start(bf16[128,2048]{1,0:T(8,128)(2,1)} %param.16) | copy-start | bytes 1572868
  109.4 2.6 %copy-start.1 = (f32[8,128,256]{2,1,0:T(8,128)S(1)}, f32[8,128,256]{2,1,0:T(8,128)}, u32[]{:S(2)}) copy-start(f32[8,128,256]{2,1,0:T(8,128)} %copy-done) | copy-start | bytes 3145732
  109.8 9.2 %copy-start.15 = (f32[2048]{0:T(1024)S(1)}, f32[2048]{0:T(1024)}, u32[]{:S(2)}) copy-start(f32[2048]{0:T(1024)} %param.26) | copy-start | bytes 24580
  109.8 9.1 %collective-permute-start.14 = (f32[1,128]{1,0:T(1,128)S(1)}, f32[1,128]{1,0:T(1,128)S(1)}, u32[]{:S(2)}, u32[]{:S(2)}) collective-permute-start(f32[1,128]{1,0:T(1,128)S(1)} %bitcast.101), channel_id=1, source_target_pairs={{0,3},{1,2},{2,1},{3,0},{4,7},{5,6},{6,5},{7,4},{8,11},{9,10},{10,... | collective-permute-start | bytes 1544 | tf_op jit(solution)/shard_map/ppermute | solution.py:324
  110.1 8.8 %collective-permute-start.13 = (f32[1,128]{1,0:T(1,128)S(1)}, f32[1,128]{1,0:T(1,128)S(1)}, u32[]{:S(2)}, u32[]{:S(2)}) collective-permute-start(f32[1,128]{1,0:T(1,128)S(1)} %bitcast.102), channel_id=1, source_target_pairs={{0,2},{1,3},{2,0},{3,1},{4,6},{5,7},{6,4},{7,5},{8,10},{9,11},{10,... | collective-permute-start | bytes 1544 | tf_op jit(solution)/shard_map/ppermute | solution.py:324
  110.2 8.7 %collective-permute-start.12 = (f32[1,128]{1,0:T(1,128)S(1)}, f32[1,128]{1,0:T(1,128)S(1)}, u32[]{:S(2)}, u32[]{:S(2)}) collective-permute-start(f32[1,128]{1,0:T(1,128)S(1)} %bitcast.103), channel_id=1, source_target_pairs={{0,1},{1,0},{2,3},{3,2},{4,5},{5,4},{6,7},{7,6},{8,9},{9,8},{10,11... | collective-permute-start | bytes 1544 | tf_op jit(solution)/shard_map/ppermute | solution.py:324
  118.5 9.8 %collective-permute-start.17 = (bf16[128,1024]{1,0:T(8,128)(2,1)S(1)}, bf16[128,1024]{1,0:T(8,128)(2,1)S(1)}, u32[]{:S(2)}, u32[]{:S(2)}) collective-permute-start(bf16[128,1024]{1,0:T(8,128)(2,1)S(1)} %select_bitcast_fusion), channel_id=1, source_target_pairs={{0,128},{128,0},{1,129},{129,1},{2,130},{130,2},{3,131},{131,3},{4... | collective-permute-start | bytes 786440 | tf_op jit(solution)/shard_map/ppermute | solution.py:184
  (7 other events, 6.7 us)
